TPU v7x, 256 devices: a whole 4x4x8 slice. The times are simulated.
256 devices in a mesh: dp: 16 (over z, x_lo), ctx: 16 (over x_hi, y, core).
Axes of the slice: x: 4 (x_hi: 2, x_lo: 2; x = x_hi * 2 + x_lo), y: 4, z: 8, core: 2. Of those that a mesh axis runs over, the one named last changes fastest.
Arguments:
- queries: bfloat16 [16, 4096, 2048], P('dp', 'ctx'), may hold values from -100 to 100
- keys: bfloat16 [16, 4096, 512], P('dp', 'ctx'), may hold values from -4 to 4
- values: bfloat16 [16, 4096, 512], P('dp', 'ctx'), may hold values from -6 to 6
- segments: int32 [16, 4096], P('dp', 'ctx'), may hold values from 0 to 7, never falling along the last dimension, each value on 1 to 2048 neighbouring positions
Outputs:
- attended: bfloat16 [16, 4096, 2048], P('dp', 'ctx')
Inputs may be any that keep to these rules, and one draw needn't show every extreme that they name: `segments`: document numbers never fall along a packed batch, every one of the 8 documents is present, and each document has at most 2048 tokens; some document has exactly 2048.
All inputs are finite; a program needn't handle non-finite values.
Results may differ from a plain program's by a relative error of at most 0.0053.
Values may be sent and summed in bfloat16 or wider, within the bound.
A program may use at most 192 MiB of HBM per device.

v0:
```python
import jax
import jax.numpy as jnp
from jax import lax
from jax.sharding import PartitionSpec as P

HQ = 16
HK = 4
HD = 128


rope_theta = 500000.0


def copy_for_each(value, axis):
    devices = lax.axis_size(axis)
    return lax.all_to_all(
        jnp.broadcast_to(value[None], (devices, *value.shape)), axis, 0, 0, tiled=True
    )


def all_in_one(value, axis):
    leaves = jax.tree.leaves(value)
    turns = sorted(range(len(leaves)), key=lambda k: -leaves[k].size)
    width = (1, *leaves[turns[0]].shape)[-1]
    lines = [
        jnp.pad(leaves[k].reshape(-1), (0, -leaves[k].size % width)).reshape(-1, width)
        for k in turns
    ]
    both, at, found = (copy_for_each(jnp.concatenate(lines), axis), 0, {})
    for k, line in zip(turns, lines):
        slab = both[:, at : at + len(line)].reshape(len(both), -1)
        found[k] = slab[:, : leaves[k].size].reshape(-1, *leaves[k].shape)
        at += len(line)
    numbers = iter(range(len(leaves)))
    return jax.tree.map(lambda _: found[next(numbers)], value)


def folded_in_pairs(pieces, combine):
    while len(jax.tree.leaves(pieces)[0]) > 1:
        pieces = jax.vmap(combine)(
            *(jax.tree.map(lambda part: part[side::2], pieces) for side in (0, 1))
        )
    return jax.tree.map(lambda part: part[0], pieces)


def carried_in(value, axis, combine, identity):
    devices, here = (lax.axis_size(axis), lax.axis_index(axis))
    passed = jnp.arange(devices) < here

    def kept(part, zero, own):
        part = jnp.where(
            passed.reshape(-1, *(1 for _ in own.shape)), part, jnp.asarray(zero, own.dtype)
        )
        return part

    pieces = all_in_one(value, axis)
    return folded_in_pairs(jax.tree.map(kept, pieces, identity, value), combine)


def from_behind(block, axis, distance):
    devices = range(lax.axis_size(axis))
    route = [(i - distance, i) for i in devices if i - distance in devices]
    return lax.ppermute(block, axis, route)


def rotate(values_in, positions, heads, head_dim):
    rows = values_in.shape[0]
    half_dim = head_dim // 2
    split = values_in.astype(jnp.float32).reshape(rows, heads, head_dim)
    inv_freq = jnp.exp(
        -jnp.log(rope_theta) * 2.0 * jnp.arange(half_dim, dtype=jnp.float32) / head_dim
    )
    angles = positions.astype(jnp.float32)[:, None] * inv_freq[None, :]
    cosine_part = jnp.cos(angles)[:, None, :]
    sine_part = jnp.sin(angles)[:, None, :]
    first_half = split[..., :half_dim]
    second_half = split[..., half_dim:]
    turned = jnp.concatenate(
        [
            first_half * cosine_part - second_half * sine_part,
            second_half * cosine_part + first_half * sine_part,
        ],
        axis=-1,
    )
    return turned.reshape(rows, heads * head_dim).astype(jnp.bfloat16)


def join_runs(earlier, later):
    joined_uniform = earlier[3] * later[3] * (earlier[1] == later[0]).astype(jnp.int32)
    joined_trail = jnp.where(
        (later[3] == 1) & (later[0] == earlier[1]), earlier[2] + later[2], later[2]
    )
    joined = (earlier[0], later[1], joined_trail, joined_uniform, jnp.int32(0))
    return tuple(
        (
            jnp.where(
                earlier[4] == 1, later_part, jnp.where(later[4] == 1, earlier_part, joined_part)
            )
            for earlier_part, later_part, joined_part in zip(earlier, later, joined)
        )
    )


def attend_piece(
    state_in, key_piece, value_piece, key_segs, key_start, query_heads, query_segs, query_index
):
    run_max, run_sum, accumulated = state_in
    width = key_piece.shape[0]
    kv_heads = query_heads.shape[1]
    head_dim = query_heads.shape[3]
    key_heads = key_piece.reshape(width, kv_heads, head_dim)
    value_heads = value_piece.reshape(width, kv_heads, head_dim)
    key_index = key_start + jnp.arange(width, dtype=jnp.int32)
    live_mask = (
        (key_segs[None, :] == query_segs[:, None])
        & (key_index[None, :] <= query_index[:, None])
        & (key_index[None, :] >= 0)
    )
    scores = jnp.einsum(
        "thgd,shd->hgts", query_heads, key_heads, preferred_element_type=jnp.float32
    ) / jnp.sqrt(jnp.float32(head_dim))
    scores = jnp.where(live_mask, scores, jnp.float32(-1e30))
    new_max = jnp.maximum(run_max, jnp.max(scores, axis=-1))
    weights = jnp.where(live_mask, jnp.exp(scores - new_max[..., None]), jnp.float32(0.0))
    rescale = jnp.exp(run_max - new_max)
    new_sum = run_sum * rescale + jnp.sum(weights, axis=-1)
    weighted = jnp.einsum(
        "hgts,shd->thgd",
        weights.astype(jnp.bfloat16),
        value_heads,
        preferred_element_type=jnp.float32,
    )
    new_acc = accumulated * jnp.transpose(rescale, (2, 0, 1))[..., None] + weighted
    return (new_max, new_sum, new_acc)


def body(queries, keys, values, segments):
    tok_rows = segments.shape[1]
    cycle_size = lax.axis_size("ctx")
    cycle_index = lax.axis_index("ctx")
    seg_ids = segments[0]
    index_all = jnp.arange(tok_rows, dtype=jnp.int32)
    previous = jnp.concatenate([seg_ids[:1] - 1, seg_ids[:-1]])
    run_start = lax.cummax(jnp.where(seg_ids != previous, index_all, 0), axis=0)
    local_pos = index_all - run_start
    summary = (
        seg_ids[0],
        seg_ids[-1],
        jnp.int32(tok_rows) - run_start[-1],
        (seg_ids[0] == seg_ids[-1]).astype(jnp.int32),
        jnp.int32(0),
    )
    identity = (jnp.int32(0), jnp.int32(0), jnp.int32(0), jnp.int32(1), jnp.int32(1))
    prefix = carried_in(summary, "ctx", join_runs, identity)
    carried = jnp.where((prefix[4] == 0) & (prefix[1] == seg_ids[0]), prefix[2], 0)
    positions = jnp.where(run_start == 0, local_pos + carried, local_pos)
    head_dim = HD
    q_heads_all = HQ
    kv_heads = HK
    group_size = q_heads_all // kv_heads
    rot_q = rotate(queries[0], positions, q_heads_all, head_dim)
    rot_k = rotate(keys[0], positions, kv_heads, head_dim)
    query_heads = rot_q.reshape(tok_rows, kv_heads, group_size, head_dim)
    query_index = cycle_index * tok_rows + index_all
    initial = (
        jnp.full((kv_heads, group_size, tok_rows), -1e30, jnp.float32),
        jnp.zeros((kv_heads, group_size, tok_rows), jnp.float32),
        jnp.zeros((tok_rows, kv_heads, group_size, head_dim), jnp.float32),
    )
    own_state = attend_piece(
        initial,
        rot_k,
        values[0],
        seg_ids,
        cycle_index * tok_rows,
        query_heads,
        seg_ids,
        query_index,
    )

    def pass_step(step_index, loop_state):
        state_now, travelling = loop_state
        arrived = from_behind((travelling[0], travelling[1], travelling[2]), "ctx", 1)
        updated = attend_piece(
            state_now,
            arrived[0],
            arrived[1],
            arrived[2],
            (cycle_index - step_index) * tok_rows,
            query_heads,
            seg_ids,
            query_index,
        )
        return (updated, arrived)

    final_state, unused_piece = lax.fori_loop(
        1, cycle_size // 2 + 1, pass_step, (own_state, (rot_k, values[0], seg_ids))
    )
    run_max, run_sum, accumulated = final_state
    result = accumulated / jnp.transpose(run_sum, (2, 0, 1))[..., None]
    attended = result.reshape(tok_rows, q_heads_all * head_dim).astype(jnp.bfloat16)[None]
    return attended


def solution(mesh):
    placed = (P("dp", "ctx", None), P("dp", "ctx", None), P("dp", "ctx", None), P("dp", "ctx"))
    return jax.shard_map(
        body, mesh=mesh, in_specs=placed, out_specs=P("dp", "ctx", None), check_vma=False
    )
```

profile of v0, /device:TPU:6, one launch (start us, length us, event | category | flops | bytes accessed | tf_op | source)
XLA Modules:
  0.0 210.5 jit_solution(14857055039330023186)
XLA Ops:
  7.5 7.5 %all-to-all-start = ((s32[16,5,1]{1,2,0:T(1,128)}), s32[16,5,1]{1,2,0:T(1,128)S(1)}, u32[]{:S(2)}, u32[]{:S(2)}) async-start(s32[16,5,1]{1,2,0:T(1,128)} %broadcast_in_dim.111), calls=%async_computation | async-start | bytes 16384 | tf_op jit(solution)/shard_map/all_to_all | solution.py:16
  21.6 2.0 fusion.59
  42.6 2.9 %subtract_convert_fusion = (bf16[256,16,64]{2,0,1:T(8,128)(2,1)S(1)}, bf16[256,16,64]{2,0,1:T(8,128)(2,1)S(1)}) fusion(f32[256,16,64]{2,1,0:T(8,128)} %get-tuple-element.253, f32[256,16,64]{2,1,0:T(8,128)S(1)} %get-tuple-element.252, f32[256,64]{1,0:T(8,128)S(1)} %get-tuple-element.267, f32[256,64]{1,0:T(8,128)S(1)} %get-tuple-element.266), kind=kLoop, calls=%fused_computation.37 | loop fusion | flops 2097152 | bytes 3276800 | tf_op jit(solution)/shard_map/convert.3
  48.0 2.9 %bitcast_add_fusion.1 = f32[256,4,4,128]{3,0,2,1:T(8,128)} fusion(f32[4,256,256,4]{2,1,3,0:T(8,128)S(1)} %get-tuple-element.286, f32[4,4,256]{2,1,0:T(4,128)S(1)} %broadcast_maximum_fusion, pred[256,256]{0,1:T(8,128)(4,1)S(1)} %and_and_fusion.1, f32[256,4,4]{0,2,1:T(4,128)S(1)} %get-tuple-element.258, bf16[256,4,128,1]{2,1,0,3:T(4,128)(2,1)S(1)} %bitcast.140), kind=kOutput, calls=%fused_computation.29 | convolution fusion | flops 274202624 | bytes 6651904 | tf_op jit(solution)/shard_map/hgts,shd->thgd/dot_general | solution.py:127
  50.9 155.2 %while.24 = (s32[]{:T(128)}, f32[4,4,256]{2,1,0:T(4,128)S(1)}, f32[4,4,256]{2,1,0:T(4,128)S(1)}, f32[256,4,4,128]{3,0,2,1:T(8,128)}, bf16[256,512]{0,1:T(8,128)(...) while((s32[]{:T(128)}, f32[4,4,256]{2,1,0:T(4,128)S(1)}, ...), condition=%wide.region_7.8_spmd.clone, body=%wide.region_4.7_spmd.clone.sunk | while | flops 551826432 | bytes 38810448 | solution.py:196
  50.9 2.0 collective-permute-start
  52.9 3.4 %collective-permute-start.1 = (bf16[256,512]{0,1:T(8,128)(2,1)S(1)}, bf16[256,512]{0,1:T(8,128)(2,1)S(1)}, u32[]{:S(2)}, u32[]{:S(2)}) collective-permute-start(bf16[256,512]{0,1:T(8,128)(2,1)S(1)} %get-tuple-element.387), channel_id=1, source_target_pairs={{0,1},{1,2},{2,3},{3,4},{4,5},{5,6},{6,7},{7,8},{8,9},{9,10},{10,1... | collective-permute-start | bytes 786440 | tf_op jit(solution)/shard_map/while/body/eval_jaxpr/ppermute | solution.py:63
  56.3 2.0 collective-permute-start.2
  59.6 4.7 %collective-permute-done.1 = bf16[256,512]{0,1:T(8,128)(2,1)S(1)} collective-permute-done((bf16[256,512]{0,1:T(8,128)(2,1)S(1)}, bf16[256,512]{0,1:T(8,128)(2,1)S(1)}, u32[]{:S(2)}, u32[]{:S(2)}) %collective-permute-start.1) | collective-permute-done | bytes 262176 | tf_op jit(solution)/shard_map/while/body/eval_jaxpr/ppermute | solution.py:63
  67.6 1.9 bitcast_add_fusion.3
  76.7 2.7 %collective-permute-done = s32[256]{0:T(256)S(1)} collective-permute-done((s32[256]{0:T(256)S(1)}, s32[256]{0:T(256)S(1)}, u32[]{:S(2)}, u32[]{:S(2)}) %collective-permute-start) | collective-permute-done | bytes 1056 | tf_op jit(solution)/shard_map/while/body/eval_jaxpr/ppermute | solution.py:63
  79.6 4.5 %collective-permute-done.1 = bf16[256,512]{0,1:T(8,128)(2,1)S(1)} collective-permute-done((bf16[256,512]{0,1:T(8,128)(2,1)S(1)}, bf16[256,512]{0,1:T(8,128)(2,1)S(1)}, u32[]{:S(2)}, u32[]{:S(2)}) %collective-permute-start.1) | collective-permute-done | bytes 262176 | tf_op jit(solution)/shard_map/while/body/eval_jaxpr/ppermute | solution.py:63
  86.9 1.9 bitcast_add_fusion.3
  96.0 2.7 %collective-permute-done = s32[256]{0:T(256)S(1)} collective-permute-done((s32[256]{0:T(256)S(1)}, s32[256]{0:T(256)S(1)}, u32[]{:S(2)}, u32[]{:S(2)}) %collective-permute-start) | collective-permute-done | bytes 1056 | tf_op jit(solution)/shard_map/while/body/eval_jaxpr/ppermute | solution.py:63
  98.9 4.5 %collective-permute-done.1 = bf16[256,512]{0,1:T(8,128)(2,1)S(1)} collective-permute-done((bf16[256,512]{0,1:T(8,128)(2,1)S(1)}, bf16[256,512]{0,1:T(8,128)(2,1)S(1)}, u32[]{:S(2)}, u32[]{:S(2)}) %collective-permute-start.1) | collective-permute-done | bytes 262176 | tf_op jit(solution)/shard_map/while/body/eval_jaxpr/ppermute | solution.py:63
  106.2 1.9 bitcast_add_fusion.3
  115.3 2.7 %collective-permute-done = s32[256]{0:T(256)S(1)} collective-permute-done((s32[256]{0:T(256)S(1)}, s32[256]{0:T(256)S(1)}, u32[]{:S(2)}, u32[]{:S(2)}) %collective-permute-start) | collective-permute-done | bytes 1056 | tf_op jit(solution)/shard_map/while/body/eval_jaxpr/ppermute | solution.py:63
  118.2 4.5 %collective-permute-done.1 = bf16[256,512]{0,1:T(8,128)(2,1)S(1)} collective-permute-done((bf16[256,512]{0,1:T(8,128)(2,1)S(1)}, bf16[256,512]{0,1:T(8,128)(2,1)S(1)}, u32[]{:S(2)}, u32[]{:S(2)}) %collective-permute-start.1) | collective-permute-done | bytes 262176 | tf_op jit(solution)/shard_map/while/body/eval_jaxpr/ppermute | solution.py:63
  125.5 1.9 bitcast_add_fusion.3
  134.6 2.7 %collective-permute-done = s32[256]{0:T(256)S(1)} collective-permute-done((s32[256]{0:T(256)S(1)}, s32[256]{0:T(256)S(1)}, u32[]{:S(2)}, u32[]{:S(2)}) %collective-permute-start) | collective-permute-done | bytes 1056 | tf_op jit(solution)/shard_map/while/body/eval_jaxpr/ppermute | solution.py:63
  137.5 4.5 %collective-permute-done.1 = bf16[256,512]{0,1:T(8,128)(2,1)S(1)} collective-permute-done((bf16[256,512]{0,1:T(8,128)(2,1)S(1)}, bf16[256,512]{0,1:T(8,128)(2,1)S(1)}, u32[]{:S(2)}, u32[]{:S(2)}) %collective-permute-start.1) | collective-permute-done | bytes 262176 | tf_op jit(solution)/shard_map/while/body/eval_jaxpr/ppermute | solution.py:63
  144.9 1.9 bitcast_add_fusion.3
  153.9 2.7 %collective-permute-done = s32[256]{0:T(256)S(1)} collective-permute-done((s32[256]{0:T(256)S(1)}, s32[256]{0:T(256)S(1)}, u32[]{:S(2)}, u32[]{:S(2)}) %collective-permute-start) | collective-permute-done | bytes 1056 | tf_op jit(solution)/shard_map/while/body/eval_jaxpr/ppermute | solution.py:63
  156.8 4.5 %collective-permute-done.1 = bf16[256,512]{0,1:T(8,128)(2,1)S(1)} collective-permute-done((bf16[256,512]{0,1:T(8,128)(2,1)S(1)}, bf16[256,512]{0,1:T(8,128)(2,1)S(1)}, u32[]{:S(2)}, u32[]{:S(2)}) %collective-permute-start.1) | collective-permute-done | bytes 262176 | tf_op jit(solution)/shard_map/while/body/eval_jaxpr/ppermute | solution.py:63
  164.2 1.9 bitcast_add_fusion.3
  173.3 2.7 %collective-permute-done = s32[256]{0:T(256)S(1)} collective-permute-done((s32[256]{0:T(256)S(1)}, s32[256]{0:T(256)S(1)}, u32[]{:S(2)}, u32[]{:S(2)}) %collective-permute-start) | collective-permute-done | bytes 1056 | tf_op jit(solution)/shard_map/while/body/eval_jaxpr/ppermute | solution.py:63
  176.1 4.5 %collective-permute-done.1 = bf16[256,512]{0,1:T(8,128)(2,1)S(1)} collective-permute-done((bf16[256,512]{0,1:T(8,128)(2,1)S(1)}, bf16[256,512]{0,1:T(8,128)(2,1)S(1)}, u32[]{:S(2)}, u32[]{:S(2)}) %collective-permute-start.1) | collective-permute-done | bytes 262176 | tf_op jit(solution)/shard_map/while/body/eval_jaxpr/ppermute | solution.py:63
  183.5 1.9 bitcast_add_fusion.3
  192.6 2.7 %collective-permute-done = s32[256]{0:T(256)S(1)} collective-permute-done((s32[256]{0:T(256)S(1)}, s32[256]{0:T(256)S(1)}, u32[]{:S(2)}, u32[]{:S(2)}) %collective-permute-start) | collective-permute-done | bytes 1056 | tf_op jit(solution)/shard_map/while/body/eval_jaxpr/ppermute | solution.py:63
  195.4 4.5 %collective-permute-done.1 = bf16[256,512]{0,1:T(8,128)(2,1)S(1)} collective-permute-done((bf16[256,512]{0,1:T(8,128)(2,1)S(1)}, bf16[256,512]{0,1:T(8,128)(2,1)S(1)}, u32[]{:S(2)}, u32[]{:S(2)}) %collective-permute-start.1) | collective-permute-done | bytes 262176 | tf_op jit(solution)/shard_map/while/body/eval_jaxpr/ppermute | solution.py:63
  202.8 1.9 bitcast_add_fusion.3
  206.1 1.9 divide_convert_fusion
  (234 shorter events, 101.8 us)
Async XLA Ops:
  7.5 16.6 %all-to-all-start = ((s32[16,5,1]{1,2,0:T(1,128)}), s32[16,5,1]{1,2,0:T(1,128)S(1)}, u32[]{:S(2)}, u32[]{:S(2)}) async-start(s32[16,5,1]{1,2,0:T(1,128)} %broadcast_in_dim.111), calls=%async_computation | async-start | bytes 16384 | tf_op jit(solution)/shard_map/all_to_all | solution.py:16
  48.0 2.9 %copy-start.2 = (bf16[1,256,512]{1,2,0:T(8,128)(2,1)S(1)}, bf16[1,256,512]{1,2,0:T(8,128)(2,1)}, u32[]{:S(2)}) copy-start(bf16[1,256,512]{1,2,0:T(8,128)(2,1)} %copy.67) | copy-start | bytes 786436
  50.9 8.5 %collective-permute-start = (s32[256]{0:T(256)S(1)}, s32[256]{0:T(256)S(1)}, u32[]{:S(2)}, u32[]{:S(2)}) collective-permute-start(s32[256]{0:T(256)S(1)} %get-tuple-element.389), channel_id=1, source_target_pairs={{0,1},{1,2},{2,3},{3,4},{4,5},{5,6},{6,7},{7,8},{8,9},{9,10},{10,1... | collective-permute-start | bytes 3080 | tf_op jit(solution)/shard_map/while/body/eval_jaxpr/ppermute | solution.py:63
  52.9 11.3 %collective-permute-start.1 = (bf16[256,512]{0,1:T(8,128)(2,1)S(1)}, bf16[256,512]{0,1:T(8,128)(2,1)S(1)}, u32[]{:S(2)}, u32[]{:S(2)}) collective-permute-start(bf16[256,512]{0,1:T(8,128)(2,1)S(1)} %get-tuple-element.387), channel_id=1, source_target_pairs={{0,1},{1,2},{2,3},{3,4},{4,5},{5,6},{6,7},{7,8},{8,9},{9,10},{10,1... | collective-permute-start | bytes 786440 | tf_op jit(solution)/shard_map/while/body/eval_jaxpr/ppermute | solution.py:63
  56.3 11.3 %collective-permute-start.2 = (bf16[256,512]{0,1:T(8,128)(2,1)S(1)}, bf16[256,512]{0,1:T(8,128)(2,1)S(1)}, u32[]{:S(2)}, u32[]{:S(2)}) collective-permute-start(bf16[256,512]{0,1:T(8,128)(2,1)S(1)} %get-tuple-element.388), channel_id=1, source_target_pairs={{0,1},{1,2},{2,3},{3,4},{4,5},{5,6},{6,7},{7,8},{8,9},{9,10},{10,1... | collective-permute-start | bytes 786440 | tf_op jit(solution)/shard_map/while/body/eval_jaxpr/ppermute | solution.py:63
  64.2 3.4 %copy-start = (f32[256,4,4,128]{3,0,2,1:T(8,128)S(1)}, f32[256,4,4,128]{3,0,2,1:T(8,128)}, u32[]{:S(2)}) copy-start(f32[256,4,4,128]{3,0,2,1:T(8,128)} %get-tuple-element.386) | copy-start | bytes 6291460 | tf_op jit(solution)/shard_map/while
  70.9 8.5 %collective-permute-start = (s32[256]{0:T(256)S(1)}, s32[256]{0:T(256)S(1)}, u32[]{:S(2)}, u32[]{:S(2)}) collective-permute-start(s32[256]{0:T(256)S(1)} %get-tuple-element.389), channel_id=1, source_target_pairs={{0,1},{1,2},{2,3},{3,4},{4,5},{5,6},{6,7},{7,8},{8,9},{9,10},{10,1... | collective-permute-start | bytes 3080 | tf_op jit(solution)/shard_map/while/body/eval_jaxpr/ppermute | solution.py:63
  72.8 11.3 %collective-permute-start.1 = (bf16[256,512]{0,1:T(8,128)(2,1)S(1)}, bf16[256,512]{0,1:T(8,128)(2,1)S(1)}, u32[]{:S(2)}, u32[]{:S(2)}) collective-permute-start(bf16[256,512]{0,1:T(8,128)(2,1)S(1)} %get-tuple-element.387), channel_id=1, source_target_pairs={{0,1},{1,2},{2,3},{3,4},{4,5},{5,6},{6,7},{7,8},{8,9},{9,10},{10,1... | collective-permute-start | bytes 786440 | tf_op jit(solution)/shard_map/while/body/eval_jaxpr/ppermute | solution.py:63
  74.7 12.2 %collective-permute-start.2 = (bf16[256,512]{0,1:T(8,128)(2,1)S(1)}, bf16[256,512]{0,1:T(8,128)(2,1)S(1)}, u32[]{:S(2)}, u32[]{:S(2)}) collective-permute-start(bf16[256,512]{0,1:T(8,128)(2,1)S(1)} %get-tuple-element.388), channel_id=1, source_target_pairs={{0,1},{1,2},{2,3},{3,4},{4,5},{5,6},{6,7},{7,8},{8,9},{9,10},{10,1... | collective-permute-start | bytes 786440 | tf_op jit(solution)/shard_map/while/body/eval_jaxpr/ppermute | solution.py:63
  84.1 2.8 %copy-start = (f32[256,4,4,128]{3,0,2,1:T(8,128)S(1)}, f32[256,4,4,128]{3,0,2,1:T(8,128)}, u32[]{:S(2)}) copy-start(f32[256,4,4,128]{3,0,2,1:T(8,128)} %get-tuple-element.386) | copy-start | bytes 6291460 | tf_op jit(solution)/shard_map/while
  90.2 8.5 %collective-permute-start = (s32[256]{0:T(256)S(1)}, s32[256]{0:T(256)S(1)}, u32[]{:S(2)}, u32[]{:S(2)}) collective-permute-start(s32[256]{0:T(256)S(1)} %get-tuple-element.389), channel_id=1, source_target_pairs={{0,1},{1,2},{2,3},{3,4},{4,5},{5,6},{6,7},{7,8},{8,9},{9,10},{10,1... | collective-permute-start | bytes 3080 | tf_op jit(solution)/shard_map/while/body/eval_jaxpr/ppermute | solution.py:63
  92.1 11.3 %collective-permute-start.1 = (bf16[256,512]{0,1:T(8,128)(2,1)S(1)}, bf16[256,512]{0,1:T(8,128)(2,1)S(1)}, u32[]{:S(2)}, u32[]{:S(2)}) collective-permute-start(bf16[256,512]{0,1:T(8,128)(2,1)S(1)} %get-tuple-element.387), channel_id=1, source_target_pairs={{0,1},{1,2},{2,3},{3,4},{4,5},{5,6},{6,7},{7,8},{8,9},{9,10},{10,1... | collective-permute-start | bytes 786440 | tf_op jit(solution)/shard_map/while/body/eval_jaxpr/ppermute | solution.py:63
  94.0 12.2 %collective-permute-start.2 = (bf16[256,512]{0,1:T(8,128)(2,1)S(1)}, bf16[256,512]{0,1:T(8,128)(2,1)S(1)}, u32[]{:S(2)}, u32[]{:S(2)}) collective-permute-start(bf16[256,512]{0,1:T(8,128)(2,1)S(1)} %get-tuple-element.388), channel_id=1, source_target_pairs={{0,1},{1,2},{2,3},{3,4},{4,5},{5,6},{6,7},{7,8},{8,9},{9,10},{10,1... | collective-permute-start | bytes 786440 | tf_op jit(solution)/shard_map/while/body/eval_jaxpr/ppermute | solution.py:63
  103.4 2.8 %copy-start = (f32[256,4,4,128]{3,0,2,1:T(8,128)S(1)}, f32[256,4,4,128]{3,0,2,1:T(8,128)}, u32[]{:S(2)}) copy-start(f32[256,4,4,128]{3,0,2,1:T(8,128)} %get-tuple-element.386) | copy-start | bytes 6291460 | tf_op jit(solution)/shard_map/while
  109.5 8.5 %collective-permute-start = (s32[256]{0:T(256)S(1)}, s32[256]{0:T(256)S(1)}, u32[]{:S(2)}, u32[]{:S(2)}) collective-permute-start(s32[256]{0:T(256)S(1)} %get-tuple-element.389), channel_id=1, source_target_pairs={{0,1},{1,2},{2,3},{3,4},{4,5},{5,6},{6,7},{7,8},{8,9},{9,10},{10,1... | collective-permute-start | bytes 3080 | tf_op jit(solution)/shard_map/while/body/eval_jaxpr/ppermute | solution.py:63
  111.4 11.3 %collective-permute-start.1 = (bf16[256,512]{0,1:T(8,128)(2,1)S(1)}, bf16[256,512]{0,1:T(8,128)(2,1)S(1)}, u32[]{:S(2)}, u32[]{:S(2)}) collective-permute-start(bf16[256,512]{0,1:T(8,128)(2,1)S(1)} %get-tuple-element.387), channel_id=1, source_target_pairs={{0,1},{1,2},{2,3},{3,4},{4,5},{5,6},{6,7},{7,8},{8,9},{9,10},{10,1... | collective-permute-start | bytes 786440 | tf_op jit(solution)/shard_map/while/body/eval_jaxpr/ppermute | solution.py:63
  113.4 12.2 %collective-permute-start.2 = (bf16[256,512]{0,1:T(8,128)(2,1)S(1)}, bf16[256,512]{0,1:T(8,128)(2,1)S(1)}, u32[]{:S(2)}, u32[]{:S(2)}) collective-permute-start(bf16[256,512]{0,1:T(8,128)(2,1)S(1)} %get-tuple-element.388), channel_id=1, source_target_pairs={{0,1},{1,2},{2,3},{3,4},{4,5},{5,6},{6,7},{7,8},{8,9},{9,10},{10,1... | collective-permute-start | bytes 786440 | tf_op jit(solution)/shard_map/while/body/eval_jaxpr/ppermute | solution.py:63
  122.7 2.8 %copy-start = (f32[256,4,4,128]{3,0,2,1:T(8,128)S(1)}, f32[256,4,4,128]{3,0,2,1:T(8,128)}, u32[]{:S(2)}) copy-start(f32[256,4,4,128]{3,0,2,1:T(8,128)} %get-tuple-element.386) | copy-start | bytes 6291460 | tf_op jit(solution)/shard_map/while
  128.8 8.5 %collective-permute-start = (s32[256]{0:T(256)S(1)}, s32[256]{0:T(256)S(1)}, u32[]{:S(2)}, u32[]{:S(2)}) collective-permute-start(s32[256]{0:T(256)S(1)} %get-tuple-element.389), channel_id=1, source_target_pairs={{0,1},{1,2},{2,3},{3,4},{4,5},{5,6},{6,7},{7,8},{8,9},{9,10},{10,1... | collective-permute-start | bytes 3080 | tf_op jit(solution)/shard_map/while/body/eval_jaxpr/ppermute | solution.py:63
  130.7 11.3 %collective-permute-start.1 = (bf16[256,512]{0,1:T(8,128)(2,1)S(1)}, bf16[256,512]{0,1:T(8,128)(2,1)S(1)}, u32[]{:S(2)}, u32[]{:S(2)}) collective-permute-start(bf16[256,512]{0,1:T(8,128)(2,1)S(1)} %get-tuple-element.387), channel_id=1, source_target_pairs={{0,1},{1,2},{2,3},{3,4},{4,5},{5,6},{6,7},{7,8},{8,9},{9,10},{10,1... | collective-permute-start | bytes 786440 | tf_op jit(solution)/shard_map/while/body/eval_jaxpr/ppermute | solution.py:63
  132.7 12.2 %collective-permute-start.2 = (bf16[256,512]{0,1:T(8,128)(2,1)S(1)}, bf16[256,512]{0,1:T(8,128)(2,1)S(1)}, u32[]{:S(2)}, u32[]{:S(2)}) collective-permute-start(bf16[256,512]{0,1:T(8,128)(2,1)S(1)} %get-tuple-element.388), channel_id=1, source_target_pairs={{0,1},{1,2},{2,3},{3,4},{4,5},{5,6},{6,7},{7,8},{8,9},{9,10},{10,1... | collective-permute-start | bytes 786440 | tf_op jit(solution)/shard_map/while/body/eval_jaxpr/ppermute | solution.py:63
  142.0 2.8 %copy-start = (f32[256,4,4,128]{3,0,2,1:T(8,128)S(1)}, f32[256,4,4,128]{3,0,2,1:T(8,128)}, u32[]{:S(2)}) copy-start(f32[256,4,4,128]{3,0,2,1:T(8,128)} %get-tuple-element.386) | copy-start | bytes 6291460 | tf_op jit(solution)/shard_map/while
  148.1 8.5 %collective-permute-start = (s32[256]{0:T(256)S(1)}, s32[256]{0:T(256)S(1)}, u32[]{:S(2)}, u32[]{:S(2)}) collective-permute-start(s32[256]{0:T(256)S(1)} %get-tuple-element.389), channel_id=1, source_target_pairs={{0,1},{1,2},{2,3},{3,4},{4,5},{5,6},{6,7},{7,8},{8,9},{9,10},{10,1... | collective-permute-start | bytes 3080 | tf_op jit(solution)/shard_map/while/body/eval_jaxpr/ppermute | solution.py:63
  150.1 11.3 %collective-permute-start.1 = (bf16[256,512]{0,1:T(8,128)(2,1)S(1)}, bf16[256,512]{0,1:T(8,128)(2,1)S(1)}, u32[]{:S(2)}, u32[]{:S(2)}) collective-permute-start(bf16[256,512]{0,1:T(8,128)(2,1)S(1)} %get-tuple-element.387), channel_id=1, source_target_pairs={{0,1},{1,2},{2,3},{3,4},{4,5},{5,6},{6,7},{7,8},{8,9},{9,10},{10,1... | collective-permute-start | bytes 786440 | tf_op jit(solution)/shard_map/while/body/eval_jaxpr/ppermute | solution.py:63
  152.0 12.2 %collective-permute-start.2 = (bf16[256,512]{0,1:T(8,128)(2,1)S(1)}, bf16[256,512]{0,1:T(8,128)(2,1)S(1)}, u32[]{:S(2)}, u32[]{:S(2)}) collective-permute-start(bf16[256,512]{0,1:T(8,128)(2,1)S(1)} %get-tuple-element.388), channel_id=1, source_target_pairs={{0,1},{1,2},{2,3},{3,4},{4,5},{5,6},{6,7},{7,8},{8,9},{9,10},{10,1... | collective-permute-start | bytes 786440 | tf_op jit(solution)/shard_map/while/body/eval_jaxpr/ppermute | solution.py:63
  167.5 8.5 %collective-permute-start = (s32[256]{0:T(256)S(1)}, s32[256]{0:T(256)S(1)}, u32[]{:S(2)}, u32[]{:S(2)}) collective-permute-start(s32[256]{0:T(256)S(1)} %get-tuple-element.389), channel_id=1, source_target_pairs={{0,1},{1,2},{2,3},{3,4},{4,5},{5,6},{6,7},{7,8},{8,9},{9,10},{10,1... | collective-permute-start | bytes 3080 | tf_op jit(solution)/shard_map/while/body/eval_jaxpr/ppermute | solution.py:63
  169.4 11.3 %collective-permute-start.1 = (bf16[256,512]{0,1:T(8,128)(2,1)S(1)}, bf16[256,512]{0,1:T(8,128)(2,1)S(1)}, u32[]{:S(2)}, u32[]{:S(2)}) collective-permute-start(bf16[256,512]{0,1:T(8,128)(2,1)S(1)} %get-tuple-element.387), channel_id=1, source_target_pairs={{0,1},{1,2},{2,3},{3,4},{4,5},{5,6},{6,7},{7,8},{8,9},{9,10},{10,1... | collective-permute-start | bytes 786440 | tf_op jit(solution)/shard_map/while/body/eval_jaxpr/ppermute | solution.py:63
  171.3 12.2 %collective-permute-start.2 = (bf16[256,512]{0,1:T(8,128)(2,1)S(1)}, bf16[256,512]{0,1:T(8,128)(2,1)S(1)}, u32[]{:S(2)}, u32[]{:S(2)}) collective-permute-start(bf16[256,512]{0,1:T(8,128)(2,1)S(1)} %get-tuple-element.388), channel_id=1, source_target_pairs={{0,1},{1,2},{2,3},{3,4},{4,5},{5,6},{6,7},{7,8},{8,9},{9,10},{10,1... | collective-permute-start | bytes 786440 | tf_op jit(solution)/shard_map/while/body/eval_jaxpr/ppermute | solution.py:63
  180.7 2.8 %copy-start = (f32[256,4,4,128]{3,0,2,1:T(8,128)S(1)}, f32[256,4,4,128]{3,0,2,1:T(8,128)}, u32[]{:S(2)}) copy-start(f32[256,4,4,128]{3,0,2,1:T(8,128)} %get-tuple-element.386) | copy-start | bytes 6291460 | tf_op jit(solution)/shard_map/while
  186.8 8.5 %collective-permute-start = (s32[256]{0:T(256)S(1)}, s32[256]{0:T(256)S(1)}, u32[]{:S(2)}, u32[]{:S(2)}) collective-permute-start(s32[256]{0:T(256)S(1)} %get-tuple-element.389), channel_id=1, source_target_pairs={{0,1},{1,2},{2,3},{3,4},{4,5},{5,6},{6,7},{7,8},{8,9},{9,10},{10,1... | collective-permute-start | bytes 3080 | tf_op jit(solution)/shard_map/while/body/eval_jaxpr/ppermute | solution.py:63
  188.7 11.3 %collective-permute-start.1 = (bf16[256,512]{0,1:T(8,128)(2,1)S(1)}, bf16[256,512]{0,1:T(8,128)(2,1)S(1)}, u32[]{:S(2)}, u32[]{:S(2)}) collective-permute-start(bf16[256,512]{0,1:T(8,128)(2,1)S(1)} %get-tuple-element.387), channel_id=1, source_target_pairs={{0,1},{1,2},{2,3},{3,4},{4,5},{5,6},{6,7},{7,8},{8,9},{9,10},{10,1... | collective-permute-start | bytes 786440 | tf_op jit(solution)/shard_map/while/body/eval_jaxpr/ppermute | solution.py:63
  190.6 12.2 %collective-permute-start.2 = (bf16[256,512]{0,1:T(8,128)(2,1)S(1)}, bf16[256,512]{0,1:T(8,128)(2,1)S(1)}, u32[]{:S(2)}, u32[]{:S(2)}) collective-permute-start(bf16[256,512]{0,1:T(8,128)(2,1)S(1)} %get-tuple-element.388), channel_id=1, source_target_pairs={{0,1},{1,2},{2,3},{3,4},{4,5},{5,6},{6,7},{7,8},{8,9},{9,10},{10,1... | collective-permute-start | bytes 786440 | tf_op jit(solution)/shard_map/while/body/eval_jaxpr/ppermute | solution.py:63
  (12 other events, 20.3 us)
where the time goes:
time: 212 us; the launch traced here: 210 us
  waiting for transfers between devices  63.6 us (30%)
  starting transfers between devices  55.1 us (26%)
  local copies, waits for them, and re-layouts  32.1 us (15%)
  matrix products  26.1 us (12%)
  other arithmetic  20.2 us (10%)
  between operations  12.4 us (6%)
    ppermute x24, waiting for transfers between devices, from_behind(): return lax.ppermute(block, axis, route)  63.6 us
    ppermute x24, starting transfers between devices, from_behind(): return lax.ppermute(block, axis, route)  47.7 us
    dot_general x9, matrix products, attend_piece(): jnp.einsum('hgts,shd->thgd', weights.astype(jnp.bfloat16), value_heads, p...  18.2 us
    while x64, local copies, waits for them, and re-layouts  10.7 us
    reduce_sum x9, other arithmetic, attend_piece(): new_sum = run_sum * rescale + jnp.sum(weights, axis=-1)  9.29 us
    dot_general x9, matrix products, attend_piece(): jnp.einsum('thgd,shd->hgts', query_heads, key_heads, preferred_element_ty...  7.85 us
    all_to_all x1, starting transfers between devices, copy_for_each(): lax.all_to_all(jnp.broadcast_to(value[None], (devices, *value.shape)), ax...  7.45 us
    slice x35, local copies, waits for them, and re-layouts, folded_in_pairs(): part[side::2]  5.85 us
  transfers between devices with their start and end apart: 25, of which 24 were waited for; matrix products, arithmetic and copies ran while one was open for 12% of the time, Pallas kernels for 0%

commit v1 on v0

v1 whole, which is shorter than its diff:
```python
import functools

import jax
import jax.numpy as jnp
from jax import lax
from jax.experimental import pallas as pl
from jax.experimental.pallas import tpu as pltpu
from jax.sharding import PartitionSpec as P

HQ = 16
HK = 4
HD = 128
GROUP = HQ // HK
HALF = HD // 2
ROWS = 256
NBACK = 8
THETA = 500000.0
DEAD = 1048576.0
MESH = pl.DeviceIdType.MESH


def cos_sin(angle):
    n = jnp.floor(angle * 0.6366197723675814 + 0.5)
    r = angle - n * 1.5703125
    r = r - n * 4.837512969970703125e-4
    r = r - n * 7.54978995489188216e-8
    z = r * r
    s = r + r * z * ((-1.9515295891e-4 * z + 8.3321608736e-3) * z - 1.6666654611e-1)
    c = 1.0 - 0.5 * z + z * z * (
        (2.443315711809948e-5 * z - 1.388731625493765e-3) * z + 4.166664568298827e-2
    )
    quarter = n.astype(jnp.int32) & 3
    odd = (quarter & 1) == 1
    cos_mag = jnp.where(odd, s, c)
    sin_mag = jnp.where(odd, c, s)
    cos = jnp.where((quarter == 1) | (quarter == 2), -cos_mag, cos_mag)
    sin = jnp.where(quarter >= 2, -sin_mag, sin_mag)
    return cos, sin


def rotated(block_t, cos, sin):
    wide = block_t.astype(jnp.float32)
    first, second = wide[:HALF], wide[HALF:]
    return jnp.concatenate(
        [first * cos - second * sin, second * cos + first * sin], axis=0
    ).astype(jnp.bfloat16)


def kernel(
    q_hbm, k_hbm, v_hbm, seg_hbm, out_ref,
    q_raw, k_raw, buf, segs, q_t, m_buf, e_buf, cos_buf, sin_buf, acc, top, total,
    in_sem, recv_sem, seg_recv, seg_send, y_send, x_send, d_send,
):
    d = lax.axis_index("ctx")
    core = lax.rem(d, 2)
    chip = lax.div(d, 2)
    col = lax.div(chip, 4)
    y = lax.rem(chip, 4)
    sibling = d + 1 - 2 * core
    scale = float(HD) ** -0.5 * 1.4426950408889634

    own = [
        pltpu.make_async_copy(seg_hbm, segs.at[0], in_sem.at[0]),
        pltpu.make_async_copy(k_hbm.at[0], k_raw, in_sem.at[1]),
        pltpu.make_async_copy(q_hbm.at[0], q_raw, in_sem.at[2]),
    ] + [
        pltpu.make_async_copy(
            v_hbm.at[0, :, pl.ds(h * HD, HD)], buf.at[0, HK + h], in_sem.at[3 + h]
        )
        for h in range(HK)
    ]
    for copy in own:
        copy.start()
    for j in range(1, NBACK + 1):
        segs[j] = jnp.full((1, ROWS), -1, jnp.int32)

    barrier = pltpu.get_barrier_semaphore()
    for k in range(1, 16):
        pl.semaphore_signal(
            barrier, inc=1, device_id={"ctx": lax.rem(d + k, 16)}, device_id_type=MESH
        )
    own[0].wait()
    for h in range(HK):
        own[3 + h].wait()
    pl.semaphore_wait(barrier, 15)

    def y_copy(src_slot, step, t):
        target = col * 8 + lax.rem(y + step, 4) * 2 + core
        return pltpu.make_async_remote_copy(
            buf.at[src_slot, t], buf.at[2 * step, t],
            y_send.at[step - 1, t], recv_sem.at[2 * step, t],
            device_id={"ctx": target}, device_id_type=MESH,
        )

    def x_copy(t):
        return pltpu.make_async_remote_copy(
            buf.at[0, t], buf.at[8, t], x_send.at[t], recv_sem.at[8, t],
            device_id={"ctx": lax.rem(d + 8, 16)}, device_id_type=MESH,
        )

    def d_copy(k, t):
        slot = 2 * k + 1 - 2 * core
        return pltpu.make_async_remote_copy(
            buf.at[2 * k, t], buf.at[slot, t], d_send.at[k, t], recv_sem.at[slot, t],
            device_id={"ctx": sibling}, device_id_type=MESH,
        )

    def seg_copy(j):
        return pltpu.make_async_remote_copy(
            segs.at[0], segs.at[j], seg_send.at[j], seg_recv.at[j],
            device_id={"ctx": lax.rem(d + j, 16)}, device_id_type=MESH,
        )

    def send_own(t, steps, others):
        for step in steps:
            @pl.when(y + step < 4)
            def _():
                y_copy(0, step, t).start()
        if others:
            @pl.when(chip < 4)
            def _():
                x_copy(t).start()

            @pl.when(core == 0)
            def _():
                d_copy_own(t).start()

    def d_copy_own(t):
        return pltpu.make_async_remote_copy(
            buf.at[0, t], buf.at[1, t], d_send.at[0, t], recv_sem.at[1, t],
            device_id={"ctx": sibling}, device_id_type=MESH,
        )

    for j in range(1, NBACK + 1):
        @pl.when(d + j < 16)
        def _():
            seg_copy(j).start()

    for h in range(HK):
        send_own(HK + h, (1, 3), True)

    for j in range(1, NBACK + 1):
        @pl.when(d >= j)
        def _():
            seg_copy(j).wait_recv()
    seg = segs[0]
    lane = lax.broadcasted_iota(jnp.int32, (1, ROWS), 1).astype(jnp.float32)
    first = jnp.min(seg.astype(jnp.float32), axis=1, keepdims=True)
    seg_f = seg.astype(jnp.float32)
    same = jnp.zeros((1, ROWS), jnp.float32)
    for j in range(1, NBACK + 1):
        same += jnp.where(segs[j].astype(jnp.float32) == first, 1.0, 0.0)
    carried = jnp.sum(same, axis=1, keepdims=True)
    start = jnp.zeros((1, ROWS), jnp.float32)
    for s in range(1, 8):
        before = jnp.sum(jnp.where(seg_f < float(s), 1.0, 0.0), axis=1, keepdims=True)
        start += jnp.where(seg_f == float(s), before, 0.0)
    pos = lane - start + jnp.where(seg_f == first, carried, 0.0)

    freq_index = lax.broadcasted_iota(jnp.int32, (HALF, ROWS), 0).astype(jnp.float32)
    inv_freq = jnp.exp(-jnp.log(jnp.float32(THETA)) * 2.0 * freq_index / HD)
    cos, sin = cos_sin(pos * inv_freq)
    cos_buf[...] = cos
    sin_buf[...] = sin

    own[1].wait()
    for h in range(HK):
        k_t = k_raw[:, h * HD : (h + 1) * HD].T
        buf[0, h] = rotated(k_t, cos, sin).T

    doc = lax.broadcasted_iota(jnp.int32, (HD, ROWS), 0)
    e_buf[...] = jnp.where(doc == seg, 1.0, 0.0).astype(jnp.bfloat16)

    def build_mask(j, carry):
        m_t = jnp.where(doc == segs[j], 0.0, -DEAD).astype(jnp.bfloat16)
        m_buf[j] = m_t.T
        return carry

    lax.fori_loop(0, NBACK + 1, build_mask, 0)

    for h in range(HK):
        send_own(h, (1, 3), True)
    for h in range(HK):
        send_own(HK + h, (2,), False)
        send_own(h, (2,), False)

    def wait_in(slot, t):
        pltpu.make_async_remote_copy(
            buf.at[slot, t], buf.at[slot, t], d_send.at[0, t], recv_sem.at[slot, t],
            device_id={"ctx": sibling}, device_id_type=MESH,
        ).wait_recv()

    def serve(k, t):
        @pl.when(chip >= k)
        def _():
            wait_in(2 * k, t)
            if k == 4:
                for step in (1, 3):
                    @pl.when(y + step >= 4)
                    def _():
                        y_copy(8, step, t).start()

                @pl.when(core == 1)
                def _():
                    d_copy(k, t).start()
            else:
                d_copy(k, t).start()

    def attend(slot, h, is_own):
        keys = jnp.concatenate([buf[slot, h], m_buf[slot]], axis=1)
        vals = buf[slot, HK + h].T
        for g in range(GROUP):
            n = h * GROUP + g
            quer = jnp.concatenate([q_t[n], e_buf[...]], axis=0)
            s = jnp.dot(keys, quer, preferred_element_type=jnp.float32)
            if is_own:
                later = lax.broadcasted_iota(jnp.int32, (ROWS, ROWS), 0) > (
                    lax.broadcasted_iota(jnp.int32, (ROWS, ROWS), 1)
                )
                s = jnp.where(later, -DEAD, s)
            peak = jnp.max(s, axis=0, keepdims=True)
            if not is_own:
                old = top[n]
                peak = jnp.maximum(old, peak)
                fade = jnp.exp2((old - peak) * scale)
            p = jnp.exp2((s - peak) * scale)
            part = jnp.sum(p, axis=0, keepdims=True)
            o = jnp.dot(vals, p.astype(jnp.bfloat16), preferred_element_type=jnp.float32)
            top[n] = peak
            if is_own:
                total[n] = part
                acc[n] = o
            else:
                total[n] = total[n] * fade + part
                acc[n] = acc[n] * fade + o

    own[2].wait()

    def own_step(h, carry):
        for g in range(GROUP):
            n = h * GROUP + g
            q_h = q_raw[:, pl.ds(pl.multiple_of(n * HD, HD), HD)]
            q_t[n] = rotated(q_h.T, cos_buf[...], sin_buf[...])
        for k in (4, 1, 3):
            serve(k, HK + h)
        attend(0, h, True)
        return carry

    lax.fori_loop(0, HK, own_step, 0)

    def near_step(h, carry):
        for k in (4, 1, 3):
            serve(k, h)

        @pl.when(core == 1)
        def _():
            wait_in(1, HK + h)
            wait_in(1, h)
            attend(1, h, False)

        for k in (4, 1, 3):
            @pl.when(chip >= k)
            def _():
                attend(2 * k, h, False)
        for k in (4, 1, 3):
            @pl.when((chip >= k) & (2 * k - 1 + 2 * core < 9))
            def _():
                slot = 2 * k - 1 + 2 * core
                wait_in(slot, HK + h)
                wait_in(slot, h)
                attend(slot, h, False)
        return carry

    def hand_far(t, carry):
        @pl.when((col == 1) & (y + 2 >= 4))
        def _():
            y_copy(8, 2, t).start()
        return carry

    def near_all(h, carry):
        near_step(h, carry)

        @pl.when(h == HK - 1)
        def _():
            lax.fori_loop(0, 2 * HK, hand_far, 0)
        return carry

    lax.fori_loop(0, HK, near_all, 0)

    def far_step(h, carry):
        serve(2, HK + h)
        serve(2, h)

        @pl.when(chip >= 2)
        def _():
            attend(4, h, False)
            slot = 3 + 2 * core
            wait_in(slot, HK + h)
            wait_in(slot, h)
            attend(slot, h, False)

        for g in range(GROUP):
            n = h * GROUP + g
            o = (acc[n] / total[n]).T
            out_ref[0, :, pl.ds(pl.multiple_of(n * HD, HD), HD)] = o.astype(jnp.bfloat16)
        return carry

    lax.fori_loop(0, HK, far_step, 0)

    for j in range(1, NBACK + 1):
        @pl.when(d + j < 16)
        def _():
            seg_copy(j).wait_send()

    def drain(t, carry):
        for step in (1, 2, 3):
            @pl.when((col == 1) | (y + step < 4))
            def _():
                y_copy(0, step, t).wait_send()

        @pl.when(chip < 4)
        def _():
            x_copy(t).wait_send()

        @pl.when(core == 0)
        def _():
            d_copy_own(t).wait_send()

        for k in (1, 2, 3):
            @pl.when(chip >= k)
            def _():
                d_copy(k, t).wait_send()

        @pl.when((chip >= 4) & (core == 1))
        def _():
            d_copy(4, t).wait_send()
        return carry

    lax.fori_loop(0, 2 * HK, drain, 0)


def body(queries, keys, values, segments):
    hbm = pl.BlockSpec(memory_space=pl.ANY)
    return pl.pallas_call(
        kernel,
        out_shape=jax.ShapeDtypeStruct((1, ROWS, HQ * HD), jnp.bfloat16),
        in_specs=[hbm] * 4,
        out_specs=pl.BlockSpec(memory_space=pltpu.VMEM),
        scratch_shapes=[
            pltpu.VMEM((ROWS, HQ * HD), jnp.bfloat16),
            pltpu.VMEM((ROWS, HK * HD), jnp.bfloat16),
            pltpu.VMEM((NBACK + 1, 2 * HK, ROWS, HD), jnp.bfloat16),
            pltpu.VMEM((NBACK + 1, 1, ROWS), jnp.int32),
            pltpu.VMEM((HQ, HD, ROWS), jnp.bfloat16),
            pltpu.VMEM((NBACK + 1, ROWS, HD), jnp.bfloat16),
            pltpu.VMEM((HD, ROWS), jnp.bfloat16),
            pltpu.VMEM((HALF, ROWS), jnp.float32),
            pltpu.VMEM((HALF, ROWS), jnp.float32),
            pltpu.VMEM((HQ, HD, ROWS), jnp.float32),
            pltpu.VMEM((HQ, 1, ROWS), jnp.float32),
            pltpu.VMEM((HQ, 1, ROWS), jnp.float32),
            pltpu.SemaphoreType.DMA((7,)),
            pltpu.SemaphoreType.DMA((NBACK + 1, 2 * HK)),
            pltpu.SemaphoreType.DMA((NBACK + 1,)),
            pltpu.SemaphoreType.DMA((NBACK + 1,)),
            pltpu.SemaphoreType.DMA((3, 2 * HK)),
            pltpu.SemaphoreType.DMA((2 * HK,)),
            pltpu.SemaphoreType.DMA((5, 2 * HK)),
        ],
        compiler_params=pltpu.CompilerParams(collective_id=0, has_side_effects=True),
    )(queries, keys, values, segments)


def solution(mesh):
    placed = (P("dp", "ctx", None), P("dp", "ctx", None), P("dp", "ctx", None), P("dp", "ctx"))
    return jax.shard_map(
        body, mesh=mesh, in_specs=placed, out_specs=P("dp", "ctx", None), check_vma=False
    )
```

time: 212 us -> 86.2 us (0.41)
  the two profiles are of different devices: /device:TPU:6 before, /device:TPU:197 now
where the time goes in v1:
time: 86.2 us; the launch traced here: 85.9 us
  Pallas kernels  83.6 us (97%)
  local copies, waits for them, and re-layouts  2.3 us (3%)
    pallas_call x1, Pallas kernels, body(): pl.pallas_call(kernel, out_shape=jax.ShapeDtypeStruct((1, ROWS, HQ * HD),...  83.6 us
    unnamed x1, local copies, waits for them, and re-layouts  2.3 us

profile of v1, /device:TPU:197, one launch (start us, length us, event | category | flops | bytes accessed | tf_op | source)
XLA Modules:
  0.0 85.9 jit_solution(15102025587995173992)
XLA Ops:
  0.0 83.6 %shard_map.46 = bf16[1,256,2048]{2,1,0:T(8,128)(2,1)} custom-call(bf16[1,256,2048]{2,1,0:T(8,128)(2,1)} %q_hbm.1, bf16[1,256,512]{2,1,0:T(8,128)(2,1)} %k_hbm.1, bf16[1,256,512]{2,1,0:T(8,128)(2,1)} %v_hbm.1, s32[1,256]{1,0:T(1,128)} %seg_hbm.1), custom_call_target="tpu_custom_call" | custom-call | tf_op jit(solution)/shard_map/pallas_call | solution.py:344
  83.6 2.3 %copy.6 = bf16[1,256,2048]{2,1,0:T(8,128)(2,1)} copy(bf16[1,256,2048]{2,1,0:T(8,128)(2,1)} %shard_map.46) | data formatting | bytes 2097152

commit v2 on v1

--- a/solution.py
+++ b/solution.py
@@ -1,5 +1,3 @@
-import functools
-
 import jax
 import jax.numpy as jnp
 from jax import lax
@@ -48,7 +46,7 @@
 
 def kernel(
     q_hbm, k_hbm, v_hbm, seg_hbm, out_ref,
-    q_raw, k_raw, buf, segs, q_t, m_buf, e_buf, cos_buf, sin_buf, acc, top, total,
+    q_raw, k_raw, buf, segs, q_t, m_buf, e_buf, cos_buf, sin_buf, acc, top, total, s_even, s_odd, p_even, p_odd,
     in_sem, recv_sem, seg_recv, seg_send, y_send, x_send, d_send,
 ):
     d = lax.axis_index("ctx")
@@ -57,6 +55,7 @@
     col = lax.div(chip, 4)
     y = lax.rem(chip, 4)
     sibling = d + 1 - 2 * core
+    s_buf, p_buf = (s_even, s_odd), (p_even, p_odd)
     scale = float(HD) ** -0.5 * 1.4426950408889634
 
     own = [
@@ -190,7 +189,7 @@
             device_id={"ctx": sibling}, device_id_type=MESH,
         ).wait_recv()
 
-    def serve(k, t):
+    def serve(k, t, far_too=None):
         @pl.when(chip >= k)
         def _():
             wait_in(2 * k, t)
@@ -199,6 +198,11 @@
                     @pl.when(y + step >= 4)
                     def _():
                         y_copy(8, step, t).start()
+                if far_too is not None:
+                    @pl.when(y >= 2)
+                    def _():
+                        for u in far_too:
+                            y_copy(8, 2, u).start()
 
                 @pl.when(core == 1)
                 def _():
@@ -206,99 +210,125 @@
             else:
                 d_copy(k, t).start()
 
-    def attend(slot, h, is_own):
-        keys = jnp.concatenate([buf[slot, h], m_buf[slot]], axis=1)
-        vals = buf[slot, HK + h].T
-        for g in range(GROUP):
+    def serve_near(t, far_too=None):
+        for k in (4, 1, 3):
+            serve(k, t, far_too)
+
+    def serve_far(h):
+        serve(2, HK + h)
+        serve(2, h)
+
+    def unit(slots, h, is_own=False):
+        width = len(slots) * ROWS
+
+        def scores(g):
             n = h * GROUP + g
             quer = jnp.concatenate([q_t[n], e_buf[...]], axis=0)
-            s = jnp.dot(keys, quer, preferred_element_type=jnp.float32)
+            peak = None if is_own else top[n]
+            for i, slot in enumerate(slots):
+                keys = jnp.concatenate([buf[slot, h], m_buf[slot]], axis=1)
+                s = jnp.dot(keys, quer, preferred_element_type=jnp.float32)
+                if is_own and i == 0:
+                    later = lax.broadcasted_iota(jnp.int32, (ROWS, ROWS), 0) > (
+                        lax.broadcasted_iota(jnp.int32, (ROWS, ROWS), 1)
+                    )
+                    s = jnp.where(later, -DEAD, s)
+                s_buf[g % 2][pl.ds(i * ROWS, ROWS)] = s
+                high = jnp.max(s, axis=0, keepdims=True)
+                peak = high if peak is None else jnp.maximum(peak, high)
+            return peak
+
+        def weigh(g, peak):
+            n = h * GROUP + g
+            fade = None if is_own else jnp.exp2((top[n] - peak) * scale)
+            top[n] = peak
+            for i in range(len(slots)):
+                p = jnp.exp2((s_buf[g % 2][pl.ds(i * ROWS, ROWS)] - peak) * scale)
+                p_buf[g % 2][pl.ds(i * ROWS, ROWS)] = p.astype(jnp.bfloat16)
+            return fade
+
+        def add_up(g, fade):
+            n = h * GROUP + g
+            vals = jnp.concatenate([buf[slot, HK + h].T for slot in slots], axis=1)
+            vals = jnp.concatenate([vals, jnp.ones((16, width), jnp.bfloat16)], axis=0)
+            o = jnp.dot(vals, p_buf[g % 2][pl.ds(0, width)], preferred_element_type=jnp.float32)
             if is_own:
-                later = lax.broadcasted_iota(jnp.int32, (ROWS, ROWS), 0) > (
-                    lax.broadcasted_iota(jnp.int32, (ROWS, ROWS), 1)
-                )
-                s = jnp.where(later, -DEAD, s)
-            peak = jnp.max(s, axis=0, keepdims=True)
-            if not is_own:
-                old = top[n]
-                peak = jnp.maximum(old, peak)
-                fade = jnp.exp2((old - peak) * scale)
-            p = jnp.exp2((s - peak) * scale)
-            part = jnp.sum(p, axis=0, keepdims=True)
-            o = jnp.dot(vals, p.astype(jnp.bfloat16), preferred_element_type=jnp.float32)
-            top[n] = peak
-            if is_own:
-                total[n] = part
-                acc[n] = o
+                acc[n] = o[:HD]
+                total[n] = o[HD : HD + 1]
             else:
-                total[n] = total[n] * fade + part
-                acc[n] = acc[n] * fade + o
+                acc[n] = acc[n] * fade + o[:HD]
+                total[n] = total[n] * fade + o[HD : HD + 1]
+
+        peaks, fades = {}, {}
+        for i in range(GROUP + 2):
+            if i < GROUP:
+                peaks[i] = scores(i)
+            if 0 <= i - 2 < GROUP:
+                add_up(i - 2, fades[i - 2])
+            if 0 <= i - 1 < GROUP:
+                fades[i - 1] = weigh(i - 1, peaks[i - 1])
+
+    def pair(k, h):
+        @pl.when(chip >= k)
+        def _():
+            slot = 2 * k - 1 + 2 * core
+
+            @pl.when(slot < 9)
+            def _():
+                wait_in(slot, HK + h)
+                wait_in(slot, h)
+                unit([2 * k, slot], h)
+
+            @pl.when(slot >= 9)
+            def _():
+                unit([2 * k], h)
 
     own[2].wait()
 
     def own_step(h, carry):
+        serve_near(HK + h)
         for g in range(GROUP):
             n = h * GROUP + g
             q_h = q_raw[:, pl.ds(pl.multiple_of(n * HD, HD), HD)]
             q_t[n] = rotated(q_h.T, cos_buf[...], sin_buf[...])
-        for k in (4, 1, 3):
-            serve(k, HK + h)
-        attend(0, h, True)
-        return carry
-
-    lax.fori_loop(0, HK, own_step, 0)
-
-    def near_step(h, carry):
-        for k in (4, 1, 3):
-            serve(k, h)
+
+        @pl.when(core == 0)
+        def _():
+            unit([0], h, True)
 
         @pl.when(core == 1)
         def _():
             wait_in(1, HK + h)
             wait_in(1, h)
-            attend(1, h, False)
-
-        for k in (4, 1, 3):
-            @pl.when(chip >= k)
-            def _():
-                attend(2 * k, h, False)
-        for k in (4, 1, 3):
-            @pl.when((chip >= k) & (2 * k - 1 + 2 * core < 9))
-            def _():
-                slot = 2 * k - 1 + 2 * core
-                wait_in(slot, HK + h)
-                wait_in(slot, h)
-                attend(slot, h, False)
+            unit([0, 1], h, True)
         return carry
 
-    def hand_far(t, carry):
-        @pl.when((col == 1) & (y + 2 >= 4))
-        def _():
-            y_copy(8, 2, t).start()
-        return carry
-
-    def near_all(h, carry):
-        near_step(h, carry)
-
+    lax.fori_loop(0, HK, own_step, 0)
+    serve_near(0, (HK, 0))
+
+    def near_step(h, carry):
+        def near_unit(i, inner):
+            pair(jnp.where(i == 0, 4, 2 * i - 1), h)
+
+            @pl.when(h == 0)
+            def _():
+                serve_near(i + 1, (HK + i + 1, i + 1))
+
+            @pl.when((h > 0) & (i == 2))
+            def _():
+                serve_far(h - 1)
+            return inner
+
+        return lax.fori_loop(0, 3, near_unit, carry)
+
+    lax.fori_loop(0, HK, near_step, 0)
+
+    def far_step(h, carry):
         @pl.when(h == HK - 1)
         def _():
-            lax.fori_loop(0, 2 * HK, hand_far, 0)
-        return carry
-
-    lax.fori_loop(0, HK, near_all, 0)
-
-    def far_step(h, carry):
-        serve(2, HK + h)
-        serve(2, h)
-
-        @pl.when(chip >= 2)
-        def _():
-            attend(4, h, False)
-            slot = 3 + 2 * core
-            wait_in(slot, HK + h)
-            wait_in(slot, h)
-            attend(slot, h, False)
-
+            serve_far(h)
+
+        pair(2, h)
         for g in range(GROUP):
             n = h * GROUP + g
             o = (acc[n] / total[n]).T
@@ -359,6 +389,10 @@
             pltpu.VMEM((HQ, HD, ROWS), jnp.float32),
             pltpu.VMEM((HQ, 1, ROWS), jnp.float32),
             pltpu.VMEM((HQ, 1, ROWS), jnp.float32),
+            pltpu.VMEM((2 * ROWS, ROWS), jnp.float32),
+            pltpu.VMEM((2 * ROWS, ROWS), jnp.float32),
+            pltpu.VMEM((2 * ROWS, ROWS), jnp.bfloat16),
+            pltpu.VMEM((2 * ROWS, ROWS), jnp.bfloat16),
             pltpu.SemaphoreType.DMA((7,)),
             pltpu.SemaphoreType.DMA((NBACK + 1, 2 * HK)),
             pltpu.SemaphoreType.DMA((NBACK + 1,)),

time: 86.2 us -> 63.5 us (0.74)
  Pallas kernels: 83.6 us -> 61.1 us
    pallas_call x1, Pallas kernels: 83.6 us -> 61.1 us  [body(): pl.pallas_call(kernel, out_shape=jax.ShapeDtypeStruct((1, ROWS, HQ * HD),...]
where the time goes in v2:
time: 63.5 us; the launch traced here: 63.4 us
  Pallas kernels  61.1 us (96%)
  local copies, waits for them, and re-layouts  2.3 us (4%)
    pallas_call x1, Pallas kernels, body(): pl.pallas_call(kernel, out_shape=jax.ShapeDtypeStruct((1, ROWS, HQ * HD),...  61.1 us
    unnamed x1, local copies, waits for them, and re-layouts  2.3 us

profile of v2, /device:TPU:197, one launch (start us, length us, event | category | flops | bytes accessed | tf_op | source)
XLA Modules:
  0.0 63.4 jit_solution(13559490946631798862)
XLA Ops:
  0.0 61.1 %shard_map.46 = bf16[1,256,2048]{2,1,0:T(8,128)(2,1)} custom-call(bf16[1,256,2048]{2,1,0:T(8,128)(2,1)} %q_hbm.1, bf16[1,256,512]{2,1,0:T(8,128)(2,1)} %k_hbm.1, bf16[1,256,512]{2,1,0:T(8,128)(2,1)} %v_hbm.1, s32[1,256]{1,0:T(1,128)} %seg_hbm.1), custom_call_target="tpu_custom_call" | custom-call | tf_op jit(solution)/shard_map/pallas_call | solution.py:374
  61.1 2.3 %copy.6 = bf16[1,256,2048]{2,1,0:T(8,128)(2,1)} copy(bf16[1,256,2048]{2,1,0:T(8,128)(2,1)} %shard_map.46) | data formatting | bytes 2097152

commit v3 on v2

--- a/solution.py
+++ b/solution.py
@@ -12,6 +12,7 @@
 HALF = HD // 2
 ROWS = 256
 NBACK = 8
+SPARE = 9
 THETA = 500000.0
 DEAD = 1048576.0
 MESH = pl.DeviceIdType.MESH
@@ -48,6 +49,7 @@
     q_hbm, k_hbm, v_hbm, seg_hbm, out_ref,
     q_raw, k_raw, buf, segs, q_t, m_buf, e_buf, cos_buf, sin_buf, acc, top, total, s_even, s_odd, p_even, p_odd,
     in_sem, recv_sem, seg_recv, seg_send, y_send, x_send, d_send,
+    r_send, f_send, s_send,
 ):
     d = lax.axis_index("ctx")
     core = lax.rem(d, 2)
@@ -83,26 +85,49 @@
         own[3 + h].wait()
     pl.semaphore_wait(barrier, 15)
 
-    def y_copy(src_slot, step, t):
-        target = col * 8 + lax.rem(y + step, 4) * 2 + core
+    def copy_to(src_slot, dst_slot, target, sem, t):
         return pltpu.make_async_remote_copy(
-            buf.at[src_slot, t], buf.at[2 * step, t],
-            y_send.at[step - 1, t], recv_sem.at[2 * step, t],
+            buf.at[src_slot, t], buf.at[dst_slot, t], sem, recv_sem.at[dst_slot, t],
             device_id={"ctx": target}, device_id_type=MESH,
         )
 
+    def ring(step):
+        return col * 8 + lax.rem(y + step, 4) * 2 + core
+
+    across = lax.rem(d + 8, 16)
+
+    def y_copy(src_slot, step, t):
+        return copy_to(src_slot, 2 * step, ring(step), y_send.at[step // 2, t], t)
+
     def x_copy(t):
-        return pltpu.make_async_remote_copy(
-            buf.at[0, t], buf.at[8, t], x_send.at[t], recv_sem.at[8, t],
-            device_id={"ctx": lax.rem(d + 8, 16)}, device_id_type=MESH,
-        )
+        return copy_to(0, 8, across, x_send.at[t], t)
+
+    def relay_up(t):
+        return copy_to(2, 4, ring(1), r_send.at[t], t)
+
+    def relay_down(t):
+        return copy_to(6, 4, ring(3), r_send.at[t], t)
+
+    def direct_far(t):
+        return copy_to(0, 4, ring(2), f_send.at[t], t)
+
+    def park(t):
+        return copy_to(0, SPARE, ring(2), f_send.at[t], t)
+
+    def cross_spare(t):
+        return copy_to(SPARE, 4, across, s_send.at[t], t)
+
+    def cross_park(t):
+        return copy_to(2, SPARE, across, s_send.at[t], t)
+
+    def wrap_spare(t):
+        return copy_to(SPARE, 4, ring(1), s_send.at[t], t)
 
     def d_copy(k, t):
-        slot = 2 * k + 1 - 2 * core
-        return pltpu.make_async_remote_copy(
-            buf.at[2 * k, t], buf.at[slot, t], d_send.at[k, t], recv_sem.at[slot, t],
-            device_id={"ctx": sibling}, device_id_type=MESH,
-        )
+        return copy_to(2 * k, 2 * k + 1 - 2 * core, sibling, d_send.at[k, t], t)
+
+    def d_copy_own(t):
+        return copy_to(0, 1, sibling, d_send.at[0, t], t)
 
     def seg_copy(j):
         return pltpu.make_async_remote_copy(
@@ -110,25 +135,30 @@
             device_id={"ctx": lax.rem(d + j, 16)}, device_id_type=MESH,
         )
 
-    def send_own(t, steps, others):
-        for step in steps:
+    def send_own(t):
+        for step in (1, 3):
             @pl.when(y + step < 4)
             def _():
                 y_copy(0, step, t).start()
-        if others:
-            @pl.when(chip < 4)
-            def _():
-                x_copy(t).start()
-
-            @pl.when(core == 0)
-            def _():
-                d_copy_own(t).start()
-
-    def d_copy_own(t):
-        return pltpu.make_async_remote_copy(
-            buf.at[0, t], buf.at[1, t], d_send.at[0, t], recv_sem.at[1, t],
-            device_id={"ctx": sibling}, device_id_type=MESH,
-        )
+
+        @pl.when(col == 0)
+        def _():
+            x_copy(t).start()
+
+        @pl.when(core == 0)
+        def _():
+            d_copy_own(t).start()
+
+    def send_far(h):
+        for t in (HK + h, h):
+            if h >= 2:
+                @pl.when(y == 1)
+                def _():
+                    direct_far(t).start()
+
+            @pl.when((col == 0) & (y == (2 if h < 2 else 3)))
+            def _():
+                park(t).start()
 
     for j in range(1, NBACK + 1):
         @pl.when(d + j < 16)
@@ -136,7 +166,7 @@
             seg_copy(j).start()
 
     for h in range(HK):
-        send_own(HK + h, (1, 3), True)
+        send_own(HK + h)
 
     for j in range(1, NBACK + 1):
         @pl.when(d >= j)
@@ -178,10 +208,9 @@
     lax.fori_loop(0, NBACK + 1, build_mask, 0)
 
     for h in range(HK):
-        send_own(h, (1, 3), True)
+        send_own(h)
     for h in range(HK):
-        send_own(HK + h, (2,), False)
-        send_own(h, (2,), False)
+        send_far(h)
 
     def wait_in(slot, t):
         pltpu.make_async_remote_copy(
@@ -189,7 +218,9 @@
             device_id={"ctx": sibling}, device_id_type=MESH,
         ).wait_recv()
 
-    def serve(k, t, far_too=None):
+    def serve(k, h, kind):
+        t = h + kind
+
         @pl.when(chip >= k)
         def _():
             wait_in(2 * k, t)
@@ -198,25 +229,37 @@
                     @pl.when(y + step >= 4)
                     def _():
                         y_copy(8, step, t).start()
-                if far_too is not None:
-                    @pl.when(y >= 2)
-                    def _():
-                        for u in far_too:
-                            y_copy(8, 2, u).start()
 
                 @pl.when(core == 1)
                 def _():
                     d_copy(k, t).start()
-            else:
-                d_copy(k, t).start()
-
-    def serve_near(t, far_too=None):
-        for k in (4, 1, 3):
-            serve(k, t, far_too)
-
-    def serve_far(h):
-        serve(2, HK + h)
-        serve(2, h)
+                return
+            if k == 1:
+                @pl.when((h < 2) & (y < 3))
+                def _():
+                    relay_up(t).start()
+
+                @pl.when((h >= 2) & (col == 0) & (y == 3))
+                def _():
+                    cross_park(t).start()
+            if k == 3:
+                @pl.when((h >= 2) & (y == 3))
+                def _():
+                    relay_down(t).start()
+            d_copy(k, t).start()
+
+    def serve_spare(h, kind):
+        t = h + kind
+
+        @pl.when((col == 0) & (y == jnp.where(h < 2, 0, 1)))
+        def _():
+            wait_in(SPARE, t)
+            cross_spare(t).start()
+
+        @pl.when((col == 1) & (y == 3) & (h >= 2))
+        def _():
+            wait_in(SPARE, t)
+            wrap_spare(t).start()
 
     def unit(slots, h, is_own=False):
         width = len(slots) * ROWS
@@ -286,11 +329,13 @@
     own[2].wait()
 
     def own_step(h, carry):
-        serve_near(HK + h)
+        serve(4, h, HK)
         for g in range(GROUP):
             n = h * GROUP + g
             q_h = q_raw[:, pl.ds(pl.multiple_of(n * HD, HD), HD)]
             q_t[n] = rotated(q_h.T, cos_buf[...], sin_buf[...])
+        serve(1, h, HK)
+        serve(3, h, HK)
 
         @pl.when(core == 0)
         def _():
@@ -304,7 +349,14 @@
         return carry
 
     lax.fori_loop(0, HK, own_step, 0)
-    serve_near(0, (HK, 0))
+
+    serve(4, 0, 0)
+    serve(1, 0, 0)
+    serve(3, 0, 0)
+
+    def spare_values(h, carry):
+        serve_spare(h, HK)
+        return carry
 
     def near_step(h, carry):
         def near_unit(i, inner):
@@ -312,11 +364,27 @@
 
             @pl.when(h == 0)
             def _():
-                serve_near(i + 1, (HK + i + 1, i + 1))
-
-            @pl.when((h > 0) & (i == 2))
-            def _():
-                serve_far(h - 1)
+                serve(4, i + 1, 0)
+                serve(1, i + 1, 0)
+                serve(3, i + 1, 0)
+
+            @pl.when((h == 0) & (i == 0))
+            def _():
+                lax.fori_loop(0, HK, spare_values, 0)
+
+            @pl.when(h == 1)
+            def _():
+                serve_spare(i, 0)
+                serve(2, i, HK)
+
+            @pl.when((h == 1) & (i == 2))
+            def _():
+                serve_spare(3, 0)
+                serve(2, 3, HK)
+
+            @pl.when((h >= 2) & (i == 2))
+            def _():
+                serve(2, h - 2, 0)
             return inner
 
         return lax.fori_loop(0, 3, near_unit, carry)
@@ -324,9 +392,9 @@
     lax.fori_loop(0, HK, near_step, 0)
 
     def far_step(h, carry):
-        @pl.when(h == HK - 1)
-        def _():
-            serve_far(h)
+        @pl.when(h < 2)
+        def _():
+            serve(2, h + 2, 0)
 
         pair(2, h)
         for g in range(GROUP):
@@ -343,14 +411,39 @@
             seg_copy(j).wait_send()
 
     def drain(t, carry):
-        for step in (1, 2, 3):
+        h = lax.rem(t, HK)
+        for step in (1, 3):
             @pl.when((col == 1) | (y + step < 4))
             def _():
                 y_copy(0, step, t).wait_send()
 
-        @pl.when(chip < 4)
+        @pl.when(col == 0)
         def _():
             x_copy(t).wait_send()
+
+        @pl.when((h < 2) & (y < 3) & (chip >= 1))
+        def _():
+            relay_up(t).wait_send()
+
+        @pl.when((h >= 2) & (y == 3))
+        def _():
+            relay_down(t).wait_send()
+
+        @pl.when((h >= 2) & (y == 1))
+        def _():
+            direct_far(t).wait_send()
+
+        @pl.when((col == 0) & (y == jnp.where(h < 2, 2, 3)))
+        def _():
+            park(t).wait_send()
+
+        @pl.when((col == 0) & (y == jnp.where(h < 2, 0, 1)))
+        def _():
+            cross_spare(t).wait_send()
+
+        @pl.when((h >= 2) & (y == 3))
+        def _():
+            cross_park(t).wait_send()
 
         @pl.when(core == 0)
         def _():
@@ -361,7 +454,7 @@
             def _():
                 d_copy(k, t).wait_send()
 
-        @pl.when((chip >= 4) & (core == 1))
+        @pl.when((col == 1) & (core == 1))
         def _():
             d_copy(4, t).wait_send()
         return carry
@@ -379,7 +472,7 @@
         scratch_shapes=[
             pltpu.VMEM((ROWS, HQ * HD), jnp.bfloat16),
             pltpu.VMEM((ROWS, HK * HD), jnp.bfloat16),
-            pltpu.VMEM((NBACK + 1, 2 * HK, ROWS, HD), jnp.bfloat16),
+            pltpu.VMEM((NBACK + 2, 2 * HK, ROWS, HD), jnp.bfloat16),
             pltpu.VMEM((NBACK + 1, 1, ROWS), jnp.int32),
             pltpu.VMEM((HQ, HD, ROWS), jnp.bfloat16),
             pltpu.VMEM((NBACK + 1, ROWS, HD), jnp.bfloat16),
@@ -394,12 +487,15 @@
             pltpu.VMEM((2 * ROWS, ROWS), jnp.bfloat16),
             pltpu.VMEM((2 * ROWS, ROWS), jnp.bfloat16),
             pltpu.SemaphoreType.DMA((7,)),
-            pltpu.SemaphoreType.DMA((NBACK + 1, 2 * HK)),
+            pltpu.SemaphoreType.DMA((NBACK + 2, 2 * HK)),
             pltpu.SemaphoreType.DMA((NBACK + 1,)),
             pltpu.SemaphoreType.DMA((NBACK + 1,)),
-            pltpu.SemaphoreType.DMA((3, 2 * HK)),
+            pltpu.SemaphoreType.DMA((2, 2 * HK)),
             pltpu.SemaphoreType.DMA((2 * HK,)),
             pltpu.SemaphoreType.DMA((5, 2 * HK)),
+            pltpu.SemaphoreType.DMA((2 * HK,)),
+            pltpu.SemaphoreType.DMA((2 * HK,)),
+            pltpu.SemaphoreType.DMA((2 * HK,)),
         ],
         compiler_params=pltpu.CompilerParams(collective_id=0, has_side_effects=True),
     )(queries, keys, values, segments)

time: 63.5 us -> 54.1 us (0.85)
  Pallas kernels: 61.1 us -> 51.7 us
    pallas_call x1, Pallas kernels: 61.1 us -> 51.7 us  [body(): pl.pallas_call(kernel, out_shape=jax.ShapeDtypeStruct((1, ROWS, HQ * HD),...]
where the time goes in v3:
time: 54.1 us; the launch traced here: 54 us
  Pallas kernels  51.7 us (96%)
  local copies, waits for them, and re-layouts  2.3 us (4%)
    pallas_call x1, Pallas kernels, body(): pl.pallas_call(kernel, out_shape=jax.ShapeDtypeStruct((1, ROWS, HQ * HD),...  51.7 us
    unnamed x1, local copies, waits for them, and re-layouts  2.3 us

profile of v3, /device:TPU:197, one launch (start us, length us, event | category | flops | bytes accessed | tf_op | source)
XLA Modules:
  0.0 54.0 jit_solution(8148022497051172725)
XLA Ops:
  0.0 51.7 %shard_map.46 = bf16[1,256,2048]{2,1,0:T(8,128)(2,1)} custom-call(bf16[1,256,2048]{2,1,0:T(8,128)(2,1)} %q_hbm.1, bf16[1,256,512]{2,1,0:T(8,128)(2,1)} %k_hbm.1, bf16[1,256,512]{2,1,0:T(8,128)(2,1)} %v_hbm.1, s32[1,256]{1,0:T(1,128)} %seg_hbm.1), custom_call_target="tpu_custom_call" | custom-call | tf_op jit(solution)/shard_map/pallas_call | solution.py:467
  51.7 2.3 %copy.6 = bf16[1,256,2048]{2,1,0:T(8,128)(2,1)} copy(bf16[1,256,2048]{2,1,0:T(8,128)(2,1)} %shard_map.46) | data formatting | bytes 2097152

commit v4 on v3

--- a/solution.py
+++ b/solution.py
@@ -13,6 +13,7 @@
 ROWS = 256
 NBACK = 8
 SPARE = 9
+VLIM = 24 << 20
 THETA = 500000.0
 DEAD = 1048576.0
 MESH = pl.DeviceIdType.MESH
@@ -46,8 +47,8 @@
 
 
 def kernel(
-    q_hbm, k_hbm, v_hbm, seg_hbm, out_ref,
-    q_raw, k_raw, buf, segs, q_t, m_buf, e_buf, cos_buf, sin_buf, acc, top, total, s_even, s_odd, p_even, p_odd,
+    q_hbm, k_hbm, v_hbm, seg_hbm, acc, total,
+    q_raw, k_raw, k_t, buf, segs, q_t, m_buf, e_buf, cos_buf, sin_buf, top, s_even, s_odd, p_even, p_odd,
     in_sem, recv_sem, seg_recv, seg_send, y_send, x_send, d_send,
     r_send, f_send, s_send,
 ):
@@ -149,16 +150,17 @@
         def _():
             d_copy_own(t).start()
 
-    def send_far(h):
-        for t in (HK + h, h):
-            if h >= 2:
-                @pl.when(y == 1)
-                def _():
-                    direct_far(t).start()
-
+    def send_parked(kind):
+        for h in range(HK):
             @pl.when((col == 0) & (y == (2 if h < 2 else 3)))
             def _():
-                park(t).start()
+                park(kind + h).start()
+
+    def send_direct(kind):
+        @pl.when(y == 1)
+        def _():
+            for h in (2, 3):
+                direct_far(kind + h).start()
 
     for j in range(1, NBACK + 1):
         @pl.when(d + j < 16)
@@ -167,6 +169,20 @@
 
     for h in range(HK):
         send_own(HK + h)
+    send_parked(HK)
+
+    own[1].wait()
+    for h in range(HK):
+        k_t[h] = k_raw[:, h * HD : (h + 1) * HD].T
+    own[2].wait()
+
+    def turn(n, carry):
+        q_t[n] = q_raw[:, pl.ds(pl.multiple_of(n * HD, HD), HD)].T
+        return carry
+
+    lax.fori_loop(0, HQ, turn, 0, unroll=4)
+    doc = lax.broadcasted_iota(jnp.int32, (HD, ROWS), 0)
+    e_buf[...] = jnp.where(doc == segs[0], 1.0, 0.0).astype(jnp.bfloat16)
 
     for j in range(1, NBACK + 1):
         @pl.when(d >= j)
@@ -192,25 +208,19 @@
     cos_buf[...] = cos
     sin_buf[...] = sin
 
-    own[1].wait()
     for h in range(HK):
-        k_t = k_raw[:, h * HD : (h + 1) * HD].T
-        buf[0, h] = rotated(k_t, cos, sin).T
-
-    doc = lax.broadcasted_iota(jnp.int32, (HD, ROWS), 0)
-    e_buf[...] = jnp.where(doc == seg, 1.0, 0.0).astype(jnp.bfloat16)
+        buf[0, h] = rotated(k_t[h], cos, sin).T
 
     def build_mask(j, carry):
         m_t = jnp.where(doc == segs[j], 0.0, -DEAD).astype(jnp.bfloat16)
         m_buf[j] = m_t.T
         return carry
 
-    lax.fori_loop(0, NBACK + 1, build_mask, 0)
-
+    lax.fori_loop(0, 2, build_mask, 0)
     for h in range(HK):
         send_own(h)
-    for h in range(HK):
-        send_far(h)
+    send_parked(0)
+    lax.fori_loop(2, NBACK + 1, build_mask, 0, unroll=7)
 
     def wait_in(slot, t):
         pltpu.make_async_remote_copy(
@@ -235,18 +245,22 @@
                     d_copy(k, t).start()
                 return
             if k == 1:
-                @pl.when((h < 2) & (y < 3))
-                def _():
-                    relay_up(t).start()
-
                 @pl.when((h >= 2) & (col == 0) & (y == 3))
                 def _():
                     cross_park(t).start()
-            if k == 3:
-                @pl.when((h >= 2) & (y == 3))
-                def _():
-                    relay_down(t).start()
             d_copy(k, t).start()
+
+    def relay():
+        for h in range(HK):
+            for t in (HK + h, h):
+                if h < 2:
+                    @pl.when((chip >= 1) & (y < 3))
+                    def _():
+                        relay_up(t).start()
+                else:
+                    @pl.when(y == 3)
+                    def _():
+                        relay_down(t).start()
 
     def serve_spare(h, kind):
         t = h + kind
@@ -261,40 +275,42 @@
             wait_in(SPARE, t)
             wrap_spare(t).start()
 
-    def unit(slots, h, is_own=False):
-        width = len(slots) * ROWS
-
-        def scores(g):
+    def pipeline(stages, ahead=None):
+        def scores(i):
+            slots, h, g, is_own = stages[i]
             n = h * GROUP + g
             quer = jnp.concatenate([q_t[n], e_buf[...]], axis=0)
             peak = None if is_own else top[n]
-            for i, slot in enumerate(slots):
+            for a, slot in enumerate(slots):
                 keys = jnp.concatenate([buf[slot, h], m_buf[slot]], axis=1)
                 s = jnp.dot(keys, quer, preferred_element_type=jnp.float32)
-                if is_own and i == 0:
+                if is_own and a == 0:
                     later = lax.broadcasted_iota(jnp.int32, (ROWS, ROWS), 0) > (
                         lax.broadcasted_iota(jnp.int32, (ROWS, ROWS), 1)
                     )
                     s = jnp.where(later, -DEAD, s)
-                s_buf[g % 2][pl.ds(i * ROWS, ROWS)] = s
+                s_buf[i % 2][pl.ds(a * ROWS, ROWS)] = s
                 high = jnp.max(s, axis=0, keepdims=True)
                 peak = high if peak is None else jnp.maximum(peak, high)
             return peak
 
-        def weigh(g, peak):
+        def weigh(i, peak):
+            slots, h, g, is_own = stages[i]
             n = h * GROUP + g
             fade = None if is_own else jnp.exp2((top[n] - peak) * scale)
             top[n] = peak
-            for i in range(len(slots)):
-                p = jnp.exp2((s_buf[g % 2][pl.ds(i * ROWS, ROWS)] - peak) * scale)
-                p_buf[g % 2][pl.ds(i * ROWS, ROWS)] = p.astype(jnp.bfloat16)
+            for a in range(len(slots)):
+                p = jnp.exp2((s_buf[i % 2][pl.ds(a * ROWS, ROWS)] - peak) * scale)
+                p_buf[i % 2][pl.ds(a * ROWS, ROWS)] = p.astype(jnp.bfloat16)
             return fade
 
-        def add_up(g, fade):
+        def add_up(i, fade):
+            slots, h, g, is_own = stages[i]
             n = h * GROUP + g
+            width = len(slots) * ROWS
             vals = jnp.concatenate([buf[slot, HK + h].T for slot in slots], axis=1)
             vals = jnp.concatenate([vals, jnp.ones((16, width), jnp.bfloat16)], axis=0)
-            o = jnp.dot(vals, p_buf[g % 2][pl.ds(0, width)], preferred_element_type=jnp.float32)
+            o = jnp.dot(vals, p_buf[i % 2][pl.ds(0, width)], preferred_element_type=jnp.float32)
             if is_own:
                 acc[n] = o[:HD]
                 total[n] = o[HD : HD + 1]
@@ -303,107 +319,184 @@
                 total[n] = total[n] * fade + o[HD : HD + 1]
 
         peaks, fades = {}, {}
-        for i in range(GROUP + 2):
-            if i < GROUP:
+        for i in range(len(stages) + 2):
+            if ahead is not None and i < len(stages) and i % GROUP == 0:
+                ahead(i // GROUP)
+            if i < len(stages):
                 peaks[i] = scores(i)
-            if 0 <= i - 2 < GROUP:
+            if i >= 2:
                 add_up(i - 2, fades[i - 2])
-            if 0 <= i - 1 < GROUP:
+            if 1 <= i <= len(stages):
                 fades[i - 1] = weigh(i - 1, peaks[i - 1])
 
-    def pair(k, h):
-        @pl.when(chip >= k)
-        def _():
-            slot = 2 * k - 1 + 2 * core
-
-            @pl.when(slot < 9)
-            def _():
-                wait_in(slot, HK + h)
-                wait_in(slot, h)
-                unit([2 * k, slot], h)
-
-            @pl.when(slot >= 9)
-            def _():
-                unit([2 * k], h)
-
-    own[2].wait()
-
-    def own_step(h, carry):
-        serve(4, h, HK)
+    def heads(slots, h, is_own=False):
+        return [(slots, h, g, is_own) for g in range(GROUP)]
+
+    def wait_both(slot, h):
+        wait_in(slot, HK + h)
+        wait_in(slot, h)
+
+    def spin(h):
         for g in range(GROUP):
             n = h * GROUP + g
-            q_h = q_raw[:, pl.ds(pl.multiple_of(n * HD, HD), HD)]
-            q_t[n] = rotated(q_h.T, cos_buf[...], sin_buf[...])
+            q_t[n] = rotated(q_t[n], cos_buf[...], sin_buf[...])
+
+    def own_step(i, carry):
+        h = 2 * i
+
+        def ahead(part):
+            if part == 1:
+                serve(4, h + 1, HK)
+
+        serve(4, h, HK)
+
+        @pl.when(i == 1)
+        def _():
+            serve(1, 1, HK)
+            serve(3, 1, HK)
+
+        spin(h)
+        spin(h + 1)
+
+        @pl.when(core == 0)
+        def _():
+            pipeline(heads([0], h, True) + heads([0], h + 1, True), ahead)
+
+        @pl.when(core == 1)
+        def _():
+            wait_both(1, h)
+            wait_both(1, h + 1)
+            pipeline(heads([0, 1], h, True) + heads([0, 1], h + 1, True), ahead)
+
         serve(1, h, HK)
         serve(3, h, HK)
-
-        @pl.when(core == 0)
-        def _():
-            unit([0], h, True)
-
-        @pl.when(core == 1)
-        def _():
-            wait_in(1, HK + h)
-            wait_in(1, h)
-            unit([0, 1], h, True)
         return carry
 
-    lax.fori_loop(0, HK, own_step, 0)
-
+    lax.fori_loop(0, HK // 2, own_step, 0)
+    send_direct(HK)
+    serve(1, 3, HK)
+    serve(3, 3, HK)
     serve(4, 0, 0)
-    serve(1, 0, 0)
-    serve(3, 0, 0)
-
-    def spare_values(h, carry):
-        serve_spare(h, HK)
+    serve(4, 1, 0)
+
+    def cross_step(i, carry):
+        h = 2 * i
+
+        def ahead_of(slot):
+            def ahead(part):
+                if slot is not None:
+                    wait_both(slot, h + part)
+                if part == 1:
+                    @pl.when(i == 0)
+                    def _():
+                        serve(4, 2, 0)
+                        serve(1, 0, 0)
+                        serve(3, 0, 0)
+            return ahead
+
+        @pl.when((col == 1) & (core == 0))
+        def _():
+            pipeline(heads([8, 7], h) + heads([8, 7], h + 1), ahead_of(7))
+
+        @pl.when((col == 1) & (core == 1))
+        def _():
+            pipeline(heads([8], h) + heads([8], h + 1), ahead_of(None))
+
+        @pl.when((col == 0) & (i == 0))
+        def _():
+            serve(1, 0, 0)
+            serve(3, 0, 0)
+
+        @pl.when(i == 0)
+        def _():
+            serve(4, 3, 0)
+            send_direct(0)
+            serve(1, 1, 0)
+            serve(3, 1, 0)
+
         return carry
 
+    lax.fori_loop(0, HK // 2, cross_step, 0)
+    serve(1, 2, 0)
+    serve(3, 2, 0)
+
     def near_step(h, carry):
-        def near_unit(i, inner):
-            pair(jnp.where(i == 0, 4, 2 * i - 1), h)
-
-            @pl.when(h == 0)
-            def _():
-                serve(4, i + 1, 0)
-                serve(1, i + 1, 0)
-                serve(3, i + 1, 0)
-
-            @pl.when((h == 0) & (i == 0))
-            def _():
-                lax.fori_loop(0, HK, spare_values, 0)
-
-            @pl.when(h == 1)
-            def _():
-                serve_spare(i, 0)
-                serve(2, i, HK)
-
-            @pl.when((h == 1) & (i == 2))
-            def _():
-                serve_spare(3, 0)
-                serve(2, 3, HK)
-
-            @pl.when((h >= 2) & (i == 2))
-            def _():
-                serve(2, h - 2, 0)
-            return inner
-
-        return lax.fori_loop(0, 3, near_unit, carry)
+        def between(part):
+            @pl.when((h == 0) & (part == 1))
+            def _():
+                serve(1, 3, 0)
+                serve(3, 3, 0)
+                relay()
+                for u in range(HK):
+                    serve_spare(u, HK)
+
+            @pl.when((h == 1) & (part == 1))
+            def _():
+                for u in range(HK):
+                    serve_spare(u, 0)
+
+            @pl.when((h == 2) & (part == 1))
+            def _():
+                serve(2, 0, HK)
+                serve(2, 0, 0)
+
+            @pl.when((h == 3) & (part == 1))
+            def _():
+                serve(2, 1, HK)
+                serve(2, 1, 0)
+
+        slots = [2 * k - 1 + 2 * core for k in (1, 3)]
+
+        @pl.when(col == 1)
+        def _():
+            def ahead(part):
+                if part == 1:
+                    between(1)
+                wait_both(slots[part], h)
+
+            pipeline(heads([2, slots[0]], h) + heads([6, slots[1]], h), ahead)
+
+        @pl.when(col == 0)
+        def _():
+            between(1)
+
+            def small(i, inner):
+                k = 2 * i + 1
+
+                @pl.when(chip >= k)
+                def _():
+                    slot = 2 * k - 1 + 2 * core
+                    wait_both(slot, h)
+                    pipeline(heads([2 * k, slot], h))
+                return inner
+
+            lax.fori_loop(0, 2, small, 0)
+
+        return carry
 
     lax.fori_loop(0, HK, near_step, 0)
 
-    def far_step(h, carry):
-        @pl.when(h < 2)
-        def _():
-            serve(2, h + 2, 0)
-
-        pair(2, h)
-        for g in range(GROUP):
-            n = h * GROUP + g
-            o = (acc[n] / total[n]).T
-            out_ref[0, :, pl.ds(pl.multiple_of(n * HD, HD), HD)] = o.astype(jnp.bfloat16)
+    def far_step(i, carry):
+        h = 2 * i
+
+        @pl.when(i == 1)
+        def _():
+            serve(2, 2, HK)
+            serve(2, 3, HK)
+            serve(2, 2, 0)
+            serve(2, 3, 0)
+
+        @pl.when(chip >= 2)
+        def _():
+            slot = 3 + 2 * core
+
+            def ahead(part):
+                wait_both(slot, h + part)
+
+            pipeline(heads([4, slot], h) + heads([4, slot], h + 1), ahead)
         return carry
 
-    lax.fori_loop(0, HK, far_step, 0)
+    lax.fori_loop(0, HK // 2, far_step, 0)
 
     for j in range(1, NBACK + 1):
         @pl.when(d + j < 16)
@@ -462,16 +555,26 @@
     lax.fori_loop(0, 2 * HK, drain, 0)
 
 
+def finish(acc, total, out):
+    for g in range(GROUP):
+        o = (acc[g] / total[g]).T
+        out[0, :, g * HD : (g + 1) * HD] = o.astype(jnp.bfloat16)
+
+
 def body(queries, keys, values, segments):
-    hbm = pl.BlockSpec(memory_space=pl.ANY)
-    return pl.pallas_call(
+    hbm = pl.BlockSpec(memory_space=pltpu.HBM)
+    acc, total = pl.pallas_call(
         kernel,
-        out_shape=jax.ShapeDtypeStruct((1, ROWS, HQ * HD), jnp.bfloat16),
+        out_shape=(
+            jax.ShapeDtypeStruct((HQ, HD, ROWS), jnp.float32),
+            jax.ShapeDtypeStruct((HQ, 1, ROWS), jnp.float32),
+        ),
         in_specs=[hbm] * 4,
-        out_specs=pl.BlockSpec(memory_space=pltpu.VMEM),
+        out_specs=(pl.BlockSpec(memory_space=pltpu.VMEM),) * 2,
         scratch_shapes=[
             pltpu.VMEM((ROWS, HQ * HD), jnp.bfloat16),
             pltpu.VMEM((ROWS, HK * HD), jnp.bfloat16),
+            pltpu.VMEM((HK, HD, ROWS), jnp.bfloat16),
             pltpu.VMEM((NBACK + 2, 2 * HK, ROWS, HD), jnp.bfloat16),
             pltpu.VMEM((NBACK + 1, 1, ROWS), jnp.int32),
             pltpu.VMEM((HQ, HD, ROWS), jnp.bfloat16),
@@ -479,8 +582,6 @@
             pltpu.VMEM((HD, ROWS), jnp.bfloat16),
             pltpu.VMEM((HALF, ROWS), jnp.float32),
             pltpu.VMEM((HALF, ROWS), jnp.float32),
-            pltpu.VMEM((HQ, HD, ROWS), jnp.float32),
-            pltpu.VMEM((HQ, 1, ROWS), jnp.float32),
             pltpu.VMEM((HQ, 1, ROWS), jnp.float32),
             pltpu.VMEM((2 * ROWS, ROWS), jnp.float32),
             pltpu.VMEM((2 * ROWS, ROWS), jnp.float32),
@@ -497,8 +598,19 @@
             pltpu.SemaphoreType.DMA((2 * HK,)),
             pltpu.SemaphoreType.DMA((2 * HK,)),
         ],
-        compiler_params=pltpu.CompilerParams(collective_id=0, has_side_effects=True),
-    )(queries, keys, values, segments)
+        compiler_params=pltpu.CompilerParams(collective_id=0, has_side_effects=True, vmem_limit_bytes=VLIM),
+    )(*(pltpu.with_memory_space_constraint(x, pltpu.HBM) for x in (queries, keys, values, segments)))
+    return pl.pallas_call(
+        finish,
+        grid=(HK,),
+        out_shape=jax.ShapeDtypeStruct((1, ROWS, HQ * HD), jnp.bfloat16),
+        in_specs=[
+            pl.BlockSpec((GROUP, HD, ROWS), lambda h: (h, 0, 0)),
+            pl.BlockSpec((GROUP, 1, ROWS), lambda h: (h, 0, 0)),
+        ],
+        out_specs=pl.BlockSpec((1, ROWS, GROUP * HD), lambda h: (0, 0, h)),
+        compiler_params=pltpu.CompilerParams(vmem_limit_bytes=8 << 20),
+    )(acc, total)
 
 
 def solution(mesh):

time: 54.1 us -> 44.3 us (0.82)
  Pallas kernels: 51.7 us -> 43.7 us
  local copies, waits for them, and re-layouts: 2.3 us -> 0 us
    pallas_call x1 -> x2, Pallas kernels: 51.7 us -> 43.7 us  [the longest x1 41.8 us: body(): pl.pallas_call(kernel, out_shape=(jax.ShapeDtypeStruct((HQ, HD, ROWS), jn...]
    unnamed x1 -> x0, local copies, waits for them, and re-layouts: 2.3 us -> none
where the time goes in v4:
time: 44.3 us; the launch traced here: 43.7 us
  Pallas kernels  43.7 us (99%)
    pallas_call x1, Pallas kernels, body(): pl.pallas_call(kernel, out_shape=(jax.ShapeDtypeStruct((HQ, HD, ROWS), jn...  41.8 us
    pallas_call x1, Pallas kernels, body(): pl.pallas_call(finish, grid=(HK,), out_shape=jax.ShapeDtypeStruct((1, ROW...  1.89 us

profile of v4, /device:TPU:197, one launch (start us, length us, event | category | flops | bytes accessed | tf_op | source)
XLA Modules:
  0.0 43.7 jit_solution(10167042226249991690)
XLA Ops:
  0.0 41.8 %shard_map.46 = (f32[16,128,256]{2,1,0:T(8,128)S(1)}, f32[16,1,256]{2,1,0:T(1,128)S(1)}) custom-call(bf16[1,256,2048]{2,1,0:T(8,128)(2,1)} %q_hbm.1, bf16[1,256,512]{2,1,0:T(8,128)(2,1)} %k_hbm.1, bf16[1,256,512]{2,1,0:T(8,128)(2,1)} %v_hbm.1, s32[1,256]{1,0:T(1,128)} %seg_hbm.1), custom_call_target="tpu_custom_call" | custom-call | tf_op jit(solution)/shard_map/pallas_call | solution.py:566
  41.8 1.9 %shard_map.47 = bf16[1,256,2048]{2,1,0:T(8,128)(2,1)} custom-call(f32[16,128,256]{2,1,0:T(8,128)S(1)} %get-tuple-element.7.acc, f32[16,1,256]{2,1,0:T(1,128)S(1)} %get-tuple-element.8.total), custom_call_target="tpu_custom_call" | custom-call | tf_op jit(solution)/shard_map/pallas_call | solution.py:603

commit v5 on v4

--- a/solution.py
+++ b/solution.py
@@ -98,37 +98,37 @@
     across = lax.rem(d + 8, 16)
 
     def y_copy(src_slot, step, t):
-        return copy_to(src_slot, 2 * step, ring(step), y_send.at[step // 2, t], t)
+        return copy_to(src_slot, 2 * step, ring(step), y_send.at[step // 2], t)
 
     def x_copy(t):
-        return copy_to(0, 8, across, x_send.at[t], t)
+        return copy_to(0, 8, across, x_send.at[0], t)
 
     def relay_up(t):
-        return copy_to(2, 4, ring(1), r_send.at[t], t)
+        return copy_to(2, 4, ring(1), r_send.at[0], t)
 
     def relay_down(t):
-        return copy_to(6, 4, ring(3), r_send.at[t], t)
+        return copy_to(6, 4, ring(3), r_send.at[0], t)
 
     def direct_far(t):
-        return copy_to(0, 4, ring(2), f_send.at[t], t)
+        return copy_to(0, 4, ring(2), f_send.at[0], t)
 
     def park(t):
-        return copy_to(0, SPARE, ring(2), f_send.at[t], t)
+        return copy_to(0, SPARE, ring(2), f_send.at[0], t)
 
     def cross_spare(t):
-        return copy_to(SPARE, 4, across, s_send.at[t], t)
+        return copy_to(SPARE, 4, across, s_send.at[0], t)
 
     def cross_park(t):
-        return copy_to(2, SPARE, across, s_send.at[t], t)
+        return copy_to(2, SPARE, across, s_send.at[0], t)
 
     def wrap_spare(t):
-        return copy_to(SPARE, 4, ring(1), s_send.at[t], t)
+        return copy_to(SPARE, 4, ring(1), s_send.at[0], t)
 
     def d_copy(k, t):
-        return copy_to(2 * k, 2 * k + 1 - 2 * core, sibling, d_send.at[k, t], t)
+        return copy_to(2 * k, 2 * k + 1 - 2 * core, sibling, d_send.at[k], t)
 
     def d_copy_own(t):
-        return copy_to(0, 1, sibling, d_send.at[0, t], t)
+        return copy_to(0, 1, sibling, d_send.at[0], t)
 
     def seg_copy(j):
         return pltpu.make_async_remote_copy(
@@ -156,11 +156,12 @@
             def _():
                 park(kind + h).start()
 
-    def send_direct(kind):
-        @pl.when(y == 1)
+    def send_direct(where):
+        @pl.when((y == 1) & (col == where))
         def _():
             for h in (2, 3):
-                direct_far(kind + h).start()
+                direct_far(HK + h).start()
+                direct_far(h).start()
 
     for j in range(1, NBACK + 1):
         @pl.when(d + j < 16)
@@ -224,7 +225,7 @@
 
     def wait_in(slot, t):
         pltpu.make_async_remote_copy(
-            buf.at[slot, t], buf.at[slot, t], d_send.at[0, t], recv_sem.at[slot, t],
+            buf.at[slot, t], buf.at[slot, t], d_send.at[0], recv_sem.at[slot, t],
             device_id={"ctx": sibling}, device_id_type=MESH,
         ).wait_recv()
 
@@ -349,12 +350,6 @@
                 serve(4, h + 1, HK)
 
         serve(4, h, HK)
-
-        @pl.when(i == 1)
-        def _():
-            serve(1, 1, HK)
-            serve(3, 1, HK)
-
         spin(h)
         spin(h + 1)
 
@@ -368,15 +363,15 @@
             wait_both(1, h + 1)
             pipeline(heads([0, 1], h, True) + heads([0, 1], h + 1, True), ahead)
 
-        serve(1, h, HK)
-        serve(3, h, HK)
         return carry
 
+    def serve_sides(h, kind):
+        serve(1, h, kind)
+        serve(3, h, kind)
+
     lax.fori_loop(0, HK // 2, own_step, 0)
-    send_direct(HK)
-    serve(1, 3, HK)
-    serve(3, 3, HK)
     serve(4, 0, 0)
+    serve_sides(0, HK)
     serve(4, 1, 0)
 
     def cross_step(i, carry):
@@ -390,8 +385,11 @@
                     @pl.when(i == 0)
                     def _():
                         serve(4, 2, 0)
-                        serve(1, 0, 0)
-                        serve(3, 0, 0)
+                        serve_sides(1, HK)
+
+                    @pl.when(i == 1)
+                    def _():
+                        serve_sides(0, 0)
             return ahead
 
         @pl.when((col == 1) & (core == 0))
@@ -404,46 +402,45 @@
 
         @pl.when((col == 0) & (i == 0))
         def _():
-            serve(1, 0, 0)
-            serve(3, 0, 0)
+            serve_sides(1, HK)
+
+        @pl.when((col == 0) & (i == 1))
+        def _():
+            serve_sides(0, 0)
 
         @pl.when(i == 0)
         def _():
             serve(4, 3, 0)
-            send_direct(0)
-            serve(1, 1, 0)
-            serve(3, 1, 0)
+            send_direct(1)
+            serve_sides(2, HK)
+            serve_sides(3, HK)
 
         return carry
 
     lax.fori_loop(0, HK // 2, cross_step, 0)
-    serve(1, 2, 0)
-    serve(3, 2, 0)
+    serve_sides(1, 0)
 
     def near_step(h, carry):
         def between(part):
             @pl.when((h == 0) & (part == 1))
             def _():
-                serve(1, 3, 0)
-                serve(3, 3, 0)
+                serve_sides(2, 0)
+                serve_sides(3, 0)
+                send_direct(0)
                 relay()
                 for u in range(HK):
                     serve_spare(u, HK)
 
-            @pl.when((h == 1) & (part == 1))
+            @pl.when((h == 1 + col) & (part == 1))
             def _():
                 for u in range(HK):
                     serve_spare(u, 0)
 
-            @pl.when((h == 2) & (part == 1))
-            def _():
-                serve(2, 0, HK)
-                serve(2, 0, 0)
-
             @pl.when((h == 3) & (part == 1))
             def _():
-                serve(2, 1, HK)
-                serve(2, 1, 0)
+                for u in (0, 1):
+                    serve(2, u, HK)
+                    serve(2, u, 0)
 
         slots = [2 * k - 1 + 2 * core for k in (1, 3)]
 
@@ -479,18 +476,18 @@
     def far_step(i, carry):
         h = 2 * i
 
-        @pl.when(i == 1)
-        def _():
-            serve(2, 2, HK)
-            serve(2, 3, HK)
-            serve(2, 2, 0)
-            serve(2, 3, 0)
-
         @pl.when(chip >= 2)
         def _():
             slot = 3 + 2 * core
 
             def ahead(part):
+                if part == 1:
+                    @pl.when(i == 0)
+                    def _():
+                        for u in (2, 3):
+                            serve(2, u, HK)
+                            serve(2, u, 0)
+
                 wait_both(slot, h + part)
 
             pipeline(heads([4, slot], h) + heads([4, slot], h + 1), ahead)
@@ -503,62 +500,51 @@
         def _():
             seg_copy(j).wait_send()
 
-    def drain(t, carry):
-        h = lax.rem(t, HK)
-        for step in (1, 3):
-            @pl.when((col == 1) | (y + step < 4))
-            def _():
-                y_copy(0, step, t).wait_send()
-
-        @pl.when(col == 0)
-        def _():
-            x_copy(t).wait_send()
-
-        @pl.when((h < 2) & (y < 3) & (chip >= 1))
-        def _():
-            relay_up(t).wait_send()
-
-        @pl.when((h >= 2) & (y == 3))
-        def _():
-            relay_down(t).wait_send()
-
-        @pl.when((h >= 2) & (y == 1))
-        def _():
-            direct_far(t).wait_send()
-
-        @pl.when((col == 0) & (y == jnp.where(h < 2, 2, 3)))
-        def _():
-            park(t).wait_send()
-
-        @pl.when((col == 0) & (y == jnp.where(h < 2, 0, 1)))
-        def _():
-            cross_spare(t).wait_send()
-
-        @pl.when((h >= 2) & (y == 3))
-        def _():
-            cross_park(t).wait_send()
-
-        @pl.when(core == 0)
-        def _():
-            d_copy_own(t).wait_send()
-
-        for k in (1, 2, 3):
-            @pl.when(chip >= k)
-            def _():
-                d_copy(k, t).wait_send()
-
-        @pl.when((col == 1) & (core == 1))
-        def _():
-            d_copy(4, t).wait_send()
-        return carry
-
-    lax.fori_loop(0, 2 * HK, drain, 0)
+    def drain(sem, chunks):
+        ref = buf.at[0, pl.ds(0, chunks)]
+        pltpu.make_async_remote_copy(
+            ref, ref, sem, recv_sem.at[0, 0], device_id={"ctx": sibling}, device_id_type=MESH
+        ).wait_send()
+
+    for step in (1, 3):
+        @pl.when((col == 1) | (y + step < 4))
+        def _():
+            drain(y_send.at[step // 2], 2 * HK)
+
+    @pl.when(col == 0)
+    def _():
+        drain(x_send.at[0], 2 * HK)
+
+    @pl.when((chip >= 1) | (y == 3))
+    def _():
+        drain(r_send.at[0], HK)
+
+    @pl.when((y == 1) | ((col == 0) & (y >= 2)))
+    def _():
+        drain(f_send.at[0], HK)
+
+    @pl.when((y == 3) | ((col == 0) & (y < 2)))
+    def _():
+        drain(s_send.at[0], HK)
+
+    @pl.when(core == 0)
+    def _():
+        drain(d_send.at[0], 2 * HK)
+
+    for k in (1, 2, 3):
+        @pl.when(chip >= k)
+        def _():
+            drain(d_send.at[k], 2 * HK)
+
+    @pl.when((col == 1) & (core == 1))
+    def _():
+        drain(d_send.at[4], 2 * HK)
 
 
 def finish(acc, total, out):
     for g in range(GROUP):
-        o = (acc[g] / total[g]).T
-        out[0, :, g * HD : (g + 1) * HD] = o.astype(jnp.bfloat16)
+        o = (acc[g] / total[g]).astype(jnp.bfloat16)
+        out[0, :, g * HD : (g + 1) * HD] = o.T
 
 
 def body(queries, keys, values, segments):
@@ -591,12 +577,12 @@
             pltpu.SemaphoreType.DMA((NBACK + 2, 2 * HK)),
             pltpu.SemaphoreType.DMA((NBACK + 1,)),
             pltpu.SemaphoreType.DMA((NBACK + 1,)),
-            pltpu.SemaphoreType.DMA((2, 2 * HK)),
-            pltpu.SemaphoreType.DMA((2 * HK,)),
-            pltpu.SemaphoreType.DMA((5, 2 * HK)),
-            pltpu.SemaphoreType.DMA((2 * HK,)),
-            pltpu.SemaphoreType.DMA((2 * HK,)),
-            pltpu.SemaphoreType.DMA((2 * HK,)),
+            pltpu.SemaphoreType.DMA((2,)),
+            pltpu.SemaphoreType.DMA((1,)),
+            pltpu.SemaphoreType.DMA((5,)),
+            pltpu.SemaphoreType.DMA((1,)),
+            pltpu.SemaphoreType.DMA((1,)),
+            pltpu.SemaphoreType.DMA((1,)),
         ],
         compiler_params=pltpu.CompilerParams(collective_id=0, has_side_effects=True, vmem_limit_bytes=VLIM),
     )(*(pltpu.with_memory_space_constraint(x, pltpu.HBM) for x in (queries, keys, values, segments)))

time: 44.3 us -> 38 us (0.86)
  Pallas kernels: 43.7 us -> 37.3 us
    pallas_call x1, Pallas kernels: 41.8 us -> 35.4 us  [body(): pl.pallas_call(kernel, out_shape=(jax.ShapeDtypeStruct((HQ, HD, ROWS), jn...]
where the time goes in v5:
time: 38 us; the launch traced here: 37.3 us
  Pallas kernels  37.3 us (98%)
    pallas_call x1, Pallas kernels, body(): pl.pallas_call(kernel, out_shape=(jax.ShapeDtypeStruct((HQ, HD, ROWS), jn...  35.4 us
    pallas_call x1, Pallas kernels, body(): pl.pallas_call(finish, grid=(HK,), out_shape=jax.ShapeDtypeStruct((1, ROW...  1.84 us

profile of v5, /device:TPU:197, one launch (start us, length us, event | category | flops | bytes accessed | tf_op | source)
XLA Modules:
  0.0 37.3 jit_solution(18054214605493261118)
XLA Ops:
  0.0 35.4 %shard_map.46 = (f32[16,128,256]{2,1,0:T(8,128)S(1)}, f32[16,1,256]{2,1,0:T(1,128)S(1)}) custom-call(bf16[1,256,2048]{2,1,0:T(8,128)(2,1)} %q_hbm.1, bf16[1,256,512]{2,1,0:T(8,128)(2,1)} %k_hbm.1, bf16[1,256,512]{2,1,0:T(8,128)(2,1)} %v_hbm.1, s32[1,256]{1,0:T(1,128)} %seg_hbm.1), custom_call_target="tpu_custom_call" | custom-call | tf_op jit(solution)/shard_map/pallas_call | solution.py:552
  35.4 1.8 %shard_map.47 = bf16[1,256,2048]{2,1,0:T(8,128)(2,1)} custom-call(f32[16,128,256]{2,1,0:T(8,128)S(1)} %get-tuple-element.7.acc, f32[16,1,256]{2,1,0:T(1,128)S(1)} %get-tuple-element.8.total), custom_call_target="tpu_custom_call" | custom-call | tf_op jit(solution)/shard_map/pallas_call | solution.py:589

commit v6 on v5

--- a/solution.py
+++ b/solution.py
@@ -49,6 +49,7 @@
 def kernel(
     q_hbm, k_hbm, v_hbm, seg_hbm, acc, total,
     q_raw, k_raw, k_t, buf, segs, q_t, m_buf, e_buf, cos_buf, sin_buf, top, s_even, s_odd, p_even, p_odd,
+    local_pos, first_doc,
     in_sem, recv_sem, seg_recv, seg_send, y_send, x_send, d_send,
     r_send, f_send, s_send,
 ):
@@ -185,27 +186,29 @@
     doc = lax.broadcasted_iota(jnp.int32, (HD, ROWS), 0)
     e_buf[...] = jnp.where(doc == segs[0], 1.0, 0.0).astype(jnp.bfloat16)
 
-    for j in range(1, NBACK + 1):
-        @pl.when(d >= j)
-        def _():
-            seg_copy(j).wait_recv()
-    seg = segs[0]
     lane = lax.broadcasted_iota(jnp.int32, (1, ROWS), 1).astype(jnp.float32)
-    first = jnp.min(seg.astype(jnp.float32), axis=1, keepdims=True)
-    seg_f = seg.astype(jnp.float32)
-    same = jnp.zeros((1, ROWS), jnp.float32)
-    for j in range(1, NBACK + 1):
-        same += jnp.where(segs[j].astype(jnp.float32) == first, 1.0, 0.0)
-    carried = jnp.sum(same, axis=1, keepdims=True)
+    seg_f = segs[0].astype(jnp.float32)
+    first = jnp.min(seg_f, axis=1, keepdims=True)
     start = jnp.zeros((1, ROWS), jnp.float32)
     for s in range(1, 8):
         before = jnp.sum(jnp.where(seg_f < float(s), 1.0, 0.0), axis=1, keepdims=True)
         start += jnp.where(seg_f == float(s), before, 0.0)
-    pos = lane - start + jnp.where(seg_f == first, carried, 0.0)
-
+    local_pos[...] = lane - start
+    first_doc[...] = jnp.broadcast_to(first, (1, ROWS))
     freq_index = lax.broadcasted_iota(jnp.int32, (HALF, ROWS), 0).astype(jnp.float32)
-    inv_freq = jnp.exp(-jnp.log(jnp.float32(THETA)) * 2.0 * freq_index / HD)
-    cos, sin = cos_sin(pos * inv_freq)
+    cos_buf[...] = jnp.exp(-jnp.log(jnp.float32(THETA)) * 2.0 * freq_index / HD)
+
+    for j in range(1, NBACK + 1):
+        @pl.when(d >= j)
+        def _():
+            seg_copy(j).wait_recv()
+    same = jnp.zeros((1, ROWS), jnp.float32)
+    for j in range(1, NBACK + 1):
+        same += jnp.where(segs[j].astype(jnp.float32) == first_doc[...], 1.0, 0.0)
+    carried = jnp.sum(same, axis=1, keepdims=True)
+    in_first = segs[0].astype(jnp.float32) == first_doc[...]
+    pos = local_pos[...] + jnp.where(in_first, carried, 0.0)
+    cos, sin = cos_sin(pos * cos_buf[...])
     cos_buf[...] = cos
     sin_buf[...] = sin
 
@@ -344,14 +347,16 @@
 
     def own_step(i, carry):
         h = 2 * i
+        spin(h)
+        spin(h + 1)
 
         def ahead(part):
             if part == 1:
                 serve(4, h + 1, HK)
 
-        serve(4, h, HK)
-        spin(h)
-        spin(h + 1)
+        @pl.when(i == 0)
+        def _():
+            serve(4, 0, HK)
 
         @pl.when(core == 0)
         def _():
@@ -363,6 +368,10 @@
             wait_both(1, h + 1)
             pipeline(heads([0, 1], h, True) + heads([0, 1], h + 1, True), ahead)
 
+        @pl.when(i == 0)
+        def _():
+            serve(4, 2, HK)
+
         return carry
 
     def serve_sides(h, kind):
@@ -371,58 +380,44 @@
 
     lax.fori_loop(0, HK // 2, own_step, 0)
     serve(4, 0, 0)
-    serve_sides(0, HK)
-    serve(4, 1, 0)
-
-    def cross_step(i, carry):
+
+    def take(part):
+        if part > 0:
+            serve(4, part, 0)
+        if part == 1:
+            serve_sides(0, HK)
+            serve_sides(1, HK)
+        if part == 2:
+            serve_sides(2, HK)
+        if part == 3:
+            send_direct(1)
+            serve_sides(3, HK)
+            serve_sides(0, 0)
+
+    @pl.when((col == 1) & (core == 0))
+    def _():
+        def ahead(part):
+            take(part)
+            wait_both(7, part)
+
+        pipeline(sum([heads([8, 7], h) for h in range(HK)], []), ahead)
+
+    @pl.when((col == 1) & (core == 1))
+    def _():
+        pipeline(sum([heads([8], h) for h in range(HK)], []), take)
+
+    @pl.when(col == 0)
+    def _():
+        for part in range(HK):
+            take(part)
+
+    serve_sides(1, 0)
+
+    def near_step(i, carry):
         h = 2 * i
 
-        def ahead_of(slot):
-            def ahead(part):
-                if slot is not None:
-                    wait_both(slot, h + part)
-                if part == 1:
-                    @pl.when(i == 0)
-                    def _():
-                        serve(4, 2, 0)
-                        serve_sides(1, HK)
-
-                    @pl.when(i == 1)
-                    def _():
-                        serve_sides(0, 0)
-            return ahead
-
-        @pl.when((col == 1) & (core == 0))
-        def _():
-            pipeline(heads([8, 7], h) + heads([8, 7], h + 1), ahead_of(7))
-
-        @pl.when((col == 1) & (core == 1))
-        def _():
-            pipeline(heads([8], h) + heads([8], h + 1), ahead_of(None))
-
-        @pl.when((col == 0) & (i == 0))
-        def _():
-            serve_sides(1, HK)
-
-        @pl.when((col == 0) & (i == 1))
-        def _():
-            serve_sides(0, 0)
-
-        @pl.when(i == 0)
-        def _():
-            serve(4, 3, 0)
-            send_direct(1)
-            serve_sides(2, HK)
-            serve_sides(3, HK)
-
-        return carry
-
-    lax.fori_loop(0, HK // 2, cross_step, 0)
-    serve_sides(1, 0)
-
-    def near_step(h, carry):
         def between(part):
-            @pl.when((h == 0) & (part == 1))
+            @pl.when((i == 0) & (part == 1))
             def _():
                 serve_sides(2, 0)
                 serve_sides(3, 0)
@@ -431,69 +426,67 @@
                 for u in range(HK):
                     serve_spare(u, HK)
 
-            @pl.when((h == 1 + col) & (part == 1))
-            def _():
-                for u in range(HK):
-                    serve_spare(u, 0)
-
-            @pl.when((h == 3) & (part == 1))
-            def _():
-                for u in (0, 1):
-                    serve(2, u, HK)
-                    serve(2, u, 0)
+            if part == 3:
+                @pl.when(i == 0)
+                def _():
+                    for u in range(HK):
+                        serve_spare(u, 0)
+
+                @pl.when((i == 1) & (col == 1))
+                def _():
+                    serve(2, 0, HK)
+                    serve(2, 0, 0)
 
         slots = [2 * k - 1 + 2 * core for k in (1, 3)]
 
         @pl.when(col == 1)
         def _():
             def ahead(part):
-                if part == 1:
-                    between(1)
-                wait_both(slots[part], h)
-
-            pipeline(heads([2, slots[0]], h) + heads([6, slots[1]], h), ahead)
+                between(part)
+                wait_both(slots[part % 2], h + part // 2)
+
+            stages = []
+            for u in (h, h + 1):
+                stages += heads([2, slots[0]], u) + heads([6, slots[1]], u)
+            pipeline(stages, ahead)
 
         @pl.when(col == 0)
         def _():
             between(1)
-
-            def small(i, inner):
-                k = 2 * i + 1
+            between(3)
+
+            def small(u, inner):
+                k = 2 * lax.rem(u, 2) + 1
 
                 @pl.when(chip >= k)
                 def _():
                     slot = 2 * k - 1 + 2 * core
-                    wait_both(slot, h)
-                    pipeline(heads([2 * k, slot], h))
+                    wait_both(slot, h + lax.div(u, 2))
+                    pipeline(heads([2 * k, slot], h + lax.div(u, 2)))
                 return inner
 
-            lax.fori_loop(0, 2, small, 0)
+            lax.fori_loop(0, 4, small, 0)
+
+            @pl.when(i == 1)
+            def _():
+                serve(2, 0, HK)
+                serve(2, 0, 0)
 
         return carry
 
-    lax.fori_loop(0, HK, near_step, 0)
-
-    def far_step(i, carry):
-        h = 2 * i
-
-        @pl.when(chip >= 2)
-        def _():
-            slot = 3 + 2 * core
-
-            def ahead(part):
-                if part == 1:
-                    @pl.when(i == 0)
-                    def _():
-                        for u in (2, 3):
-                            serve(2, u, HK)
-                            serve(2, u, 0)
-
-                wait_both(slot, h + part)
-
-            pipeline(heads([4, slot], h) + heads([4, slot], h + 1), ahead)
-        return carry
-
-    lax.fori_loop(0, HK // 2, far_step, 0)
+    lax.fori_loop(0, HK // 2, near_step, 0)
+
+    @pl.when(chip >= 2)
+    def _():
+        slot = 3 + 2 * core
+
+        def ahead(part):
+            if part < 3:
+                serve(2, part + 1, HK)
+                serve(2, part + 1, 0)
+            wait_both(slot, part)
+
+        pipeline(sum([heads([4, slot], h) for h in range(HK)], []), ahead)
 
     for j in range(1, NBACK + 1):
         @pl.when(d + j < 16)
@@ -573,6 +566,8 @@
             pltpu.VMEM((2 * ROWS, ROWS), jnp.float32),
             pltpu.VMEM((2 * ROWS, ROWS), jnp.bfloat16),
             pltpu.VMEM((2 * ROWS, ROWS), jnp.bfloat16),
+            pltpu.VMEM((1, ROWS), jnp.float32),
+            pltpu.VMEM((1, ROWS), jnp.float32),
             pltpu.SemaphoreType.DMA((7,)),
             pltpu.SemaphoreType.DMA((NBACK + 2, 2 * HK)),
             pltpu.SemaphoreType.DMA((NBACK + 1,)),

time: 38 us -> 37 us (0.974); the launches traced: 37.3 us -> 36.9 us
  Pallas kernels: 37.3 us -> 36.9 us
where the time goes in v6:
time: 37 us; the launch traced here: 36.9 us
  Pallas kernels  36.9 us (100%)
    pallas_call x1, Pallas kernels, body(): pl.pallas_call(kernel, out_shape=(jax.ShapeDtypeStruct((HQ, HD, ROWS), jn...  35.1 us
    pallas_call x1, Pallas kernels, body(): pl.pallas_call(finish, grid=(HK,), out_shape=jax.ShapeDtypeStruct((1, ROW...  1.84 us

profile of v6, /device:TPU:197, one launch (start us, length us, event | category | flops | bytes accessed | tf_op | source)
XLA Modules:
  0.0 36.9 jit_solution(442828481074552318)
XLA Ops:
  0.0 35.1 %shard_map.46 = (f32[16,128,256]{2,1,0:T(8,128)S(1)}, f32[16,1,256]{2,1,0:T(1,128)S(1)}) custom-call(bf16[1,256,2048]{2,1,0:T(8,128)(2,1)} %q_hbm.1, bf16[1,256,512]{2,1,0:T(8,128)(2,1)} %k_hbm.1, bf16[1,256,512]{2,1,0:T(8,128)(2,1)} %v_hbm.1, s32[1,256]{1,0:T(1,128)} %seg_hbm.1), custom_call_target="tpu_custom_call" | custom-call | tf_op jit(solution)/shard_map/pallas_call | solution.py:545
  35.1 1.8 %shard_map.47 = bf16[1,256,2048]{2,1,0:T(8,128)(2,1)} custom-call(f32[16,128,256]{2,1,0:T(8,128)S(1)} %get-tuple-element.7.acc, f32[16,1,256]{2,1,0:T(1,128)S(1)} %get-tuple-element.8.total), custom_call_target="tpu_custom_call" | custom-call | tf_op jit(solution)/shard_map/pallas_call | solution.py:584
